TPU v7x, 32 devices: a whole 2x2x4 slice. The times are simulated.
32 devices in a mesh: rows: 8 (over y, x, core), cols: 4 (over z).
Axes of the slice: x: 2, y: 2, z: 4, core: 2. Of those that a mesh axis runs over, the one named last changes fastest.
Arguments:
- memory: float32 [128, 262144], P('cols', 'rows'), may hold values from -3 to 3
- last_tick: int32 [262144], P('rows'), may hold values from 0 to 999
- slot_node: int32 [64, 256], P('rows'), may hold values from 0 to 262143, as said below
- slot_pair: int32 [64, 256], P('rows'), may hold values from 0 to 2047, as said below
- slot_tick: int32 [64, 256], P('rows'), may hold values from 1000 to 1999
- block_count: int32 [8, 8], P('rows'), may hold values from 0 to 256, as said below
- time_freq: float32 [128], replicated, may hold values from 0.002 to 0.1
- time_phase: float32 [128], replicated, may hold values from -3.140625 to 3.140625
- w_pair: bfloat16 [128, 2, 384], P('cols'), may hold values from -0.3125 to 0.3125
- w_time: bfloat16 [128, 384], P('cols'), may hold values from -0.3125 to 0.3125
- w_hidden: bfloat16 [128, 384], P('cols'), may hold values from -0.5 to 0.5
- bias_input: float32 [384], P('cols'), may hold values from -3 to 3
- bias_hidden: float32 [384], P('cols'), may hold values from -3 to 3
Outputs:
- new_memory: float32 [128, 262144], P('cols', 'rows')
Inputs may be any that keep to these rules, and one draw needn't show every extreme that they name: `slot_node`: every slot of block b (live or not) names a node of owner b, from b * 32768 to (b + 1) * 32768 - 1. `slot_pair`: indexes the holder's 8 * 256 slots flattened block by block; the relation is symmetric without fixed points, and live slots pair with live slots. `block_count`: every count is even; in every draw one owner's block is full (256 live slots) from every holder.
All inputs are finite; a program needn't handle non-finite values.
Results may differ from a plain program's by a relative error of at most 0.0006.
Values may be sent and summed in bfloat16 or wider, within the bound.
A program may use at most 128 MiB of HBM per device.

v0:
```python
import functools

import jax
import jax.numpy as jnp
from jax import lax
from jax.experimental import pallas as pl
from jax.experimental.pallas import tpu as pltpu
from jax.sharding import PartitionSpec as P

MESH = pl.DeviceIdType.MESH
LANES = 128
VM = pl.BlockSpec(memory_space=pltpu.VMEM)
SM = pl.BlockSpec(memory_space=pltpu.SMEM)
ANY = pl.BlockSpec(memory_space=pl.ANY)


def greet(axis, n):
    barrier = pltpu.get_barrier_semaphore()
    me = lax.axis_index(axis)
    for k in range(1, n):
        pl.semaphore_signal(
            barrier, inc=1, device_id={axis: lax.rem(me + k, n)}, device_id_type=MESH
        )


def exchange(axis, n, src, dst, send, recv):
    me = lax.axis_index(axis)
    copies = []
    for k in range(1, n):
        peer = lax.rem(me + k, n)
        copies.append(
            pltpu.make_async_remote_copy(
                src_ref=src.at[peer],
                dst_ref=dst.at[me],
                send_sem=send.at[k],
                recv_sem=recv.at[k],
                device_id={axis: peer},
                device_id_type=MESH,
            )
        )
    for copy in copies:
        copy.start()
    return copies


def first_kernel(n, c, meta, w, meta_out, w_out, ssem, rsem, wssem, wrsem):
    greet("rows", n)
    greet("cols", c)
    pl.semaphore_wait(pltpu.get_barrier_semaphore(), n + c - 2)
    copies = exchange("rows", n, meta, meta_out, ssem, rsem)
    copies += exchange("cols", c, w, w_out, wssem, wrsem)
    row, col = lax.axis_index("rows"), lax.axis_index("cols")
    meta_out[row] = meta[row]
    w_out[col] = w[col]
    for copy in copies:
        copy.wait()


def chain(c, block, first, places, sems):
    col = lax.axis_index("cols")
    n = len(places)
    ways = (True, False)

    def hop(source, t, k, right):
        send, recv = sems[0:2] if right else sems[2:4]
        ref = block(source, places[k])
        return pltpu.make_async_remote_copy(
            src_ref=first(k) if t == 0 else ref,
            dst_ref=ref,
            send_sem=send.at[t, k],
            recv_sem=recv.at[t, k],
            device_id={"cols": col + 1 if right else col - 1},
            device_id_type=MESH,
        )

    def goes(right):
        return col < c - 1 if right else col > 0

    def where_from(t, right):
        source = col - t if right else col + t
        there = source >= 0 if right else source < c
        return source, there

    def begin(k):
        for right in ways:

            @pl.when(goes(right))
            def _(right=right):
                hop(col, 0, k, right).start()

    def rest():
        for t in range(1, c):
            for k in range(n):
                for right in ways:
                    source, there = where_from(t, right)

                    @pl.when(there)
                    def _(right=right, source=source, t=t, k=k):
                        hop(source, t - 1, k, right).wait_recv()

                    @pl.when(jnp.logical_and(there, goes(right)))
                    def _(right=right, source=source, t=t, k=k):
                        hop(source, t, k, right).start()

        for t in range(c - 1):
            for right in ways:
                source, there = where_from(t, right)

                @pl.when(jnp.logical_and(there, goes(right)))
                def _(right=right, source=source, t=t):
                    for k in range(n):
                        hop(source, t, k, right).wait_send()

    return begin, rest


def reply_kernel(n, c, src, dst, self_all, ssem, rsem, *sems):
    greet("rows", n)
    greet("cols", c)
    pl.semaphore_wait(pltpu.get_barrier_semaphore(), n + c - 2)
    copies = exchange("rows", n, src, dst, ssem, rsem)
    begin, rest = chain(
        c, lambda source, k: self_all.at[source, k], lambda k: src.at[k], list(range(n)), sems
    )
    for k in range(n):
        begin(k)
    row, col = lax.axis_index("rows"), lax.axis_index("cols")
    dst[row] = src[row]
    self_all[col] = src[...]
    rest()
    for copy in copies:
        copy.wait()


def spread_kernel(n, c, perm, part_all, ssem, rsem, *sems):
    row, col = lax.axis_index("rows"), lax.axis_index("cols")
    greet("rows", n)
    greet("cols", c)
    pl.semaphore_wait(pltpu.get_barrier_semaphore(), n + c - 2)
    copies = []
    for k in range(1, n):
        peer = lax.rem(row + k, n)
        copies.append(
            pltpu.make_async_remote_copy(
                src_ref=perm.at[peer],
                dst_ref=part_all.at[col, row],
                send_sem=ssem.at[k],
                recv_sem=rsem.at[k],
                device_id={"rows": peer},
                device_id_type=MESH,
            )
        )
    for copy in copies:
        copy.start()
    places = [lax.rem(row - k + n, n) for k in range(n)]
    begin, rest = chain(
        c,
        lambda source, place: part_all.at[source, place],
        lambda k: part_all.at[col, places[k]] if k else perm.at[row],
        places,
        sems,
    )
    begin(0)
    part_all[col, row] = perm[row]
    for k in range(1, n):
        copies[k - 1].wait_recv()
        begin(k)
    rest()
    for copy in copies:
        copy.wait_send()


def prepare_kernel(nodes, ticks, counts, w_pair, w_time, w_hid, meta, w, node_rows):
    n, cap = nodes.shape
    c, _, _, g3 = w.shape
    lane = lax.broadcasted_iota(jnp.int32, (1, cap), 1)
    for b in range(n):
        mine = nodes[b : b + 1, :] - b * node_rows
        meta[b, 0:1, :] = jnp.where(lane < counts[0, b], mine, node_rows)
        meta[b, 1:2, :] = ticks[b : b + 1, :]
    width = c * g3
    kinds = (w_pair[:, 0:width], w_pair[:, width : 2 * width], w_time[...], w_hid[...])
    for k, kind in enumerate(kinds):
        for p in range(c):
            w[p, k] = kind[:, p * g3 : (p + 1) * g3]


def load_rows(wp, node_rows, pieces, memory, flat, rows, sems):
    groups = LANES // wp
    step = node_rows // pieces
    copies = []
    for i in range(pieces):
        part = pl.ds(i * step, step)
        copies.append(pltpu.make_async_copy(memory.at[:, part], flat.at[:, part], sems.at[i]))
    for copy in copies:
        copy.start()
    per_piece = step // (groups * LANES)

    def turn(q, _):
        tiles = [
            flat[:, pl.ds(pl.multiple_of((q * groups + k) * LANES, LANES), LANES)]
            for k in range(groups)
        ]
        rows[pl.ds(pl.multiple_of(q * LANES, LANES), LANES), :] = jnp.concatenate(tiles, 0).T
        return 0

    def finish():
        for i, copy in enumerate(copies):
            copy.wait()
            lax.fori_loop(i * per_piece, (i + 1) * per_piece, turn, 0, unroll=4)

    return finish


def row_of(node, groups):
    high = lax.shift_right_logical(node, 7 + groups.bit_length() - 1)
    return high * LANES + lax.bitwise_and(node, LANES - 1)


def gather_kernel(ids, meta, last, memory, own, own16, gaps, flat, rows, picked, tpicked, sems):
    wp, node_rows = memory.shape
    n, _, cap = meta.shape
    per = cap // LANES
    groups = LANES // wp
    finish = load_rows(wp, node_rows, sems.shape[0], memory, flat, rows, sems)
    finish()
    down = lax.broadcasted_iota(jnp.int32, (LANES, LANES), 0)

    def tile(i, _):
        block, half = i // per, lax.rem(i, per)
        lanes = pl.ds(pl.multiple_of(half * LANES, LANES), LANES)

        def slot(j, _):
            node = jnp.minimum(ids[block, 0, half * LANES + j], node_rows - 1)
            picked[pl.ds(j, 1), :] = rows[pl.ds(row_of(node, groups), 1), :]
            tpicked[pl.ds(j, 1), :] = last[pl.ds(lax.shift_right_logical(node, 7), 1), :]
            return 0

        lax.fori_loop(0, LANES, slot, 0, unroll=16)
        node = jnp.minimum(meta[block, 0:1, lanes], node_rows - 1)
        group = lax.bitwise_and(lax.shift_right_logical(node, 7), groups - 1)
        turned = picked[...].T
        mine = turned[0:wp]
        for k in range(1, groups):
            mine = jnp.where(group == k, turned[k * wp : (k + 1) * wp], mine)
        own[:, pl.ds(pl.multiple_of(i * LANES, LANES), LANES)] = mine
        own16[block, :, lanes] = mine.astype(jnp.bfloat16)
        old = tpicked[...].astype(jnp.float32).T
        old = jnp.where(down == lax.bitwise_and(node, LANES - 1), old, 0.0)
        old = jnp.sum(old, axis=0, keepdims=True)
        gaps[pl.ds(i, 1), :] = meta[block, 1:2, lanes].astype(jnp.float32) - old
        return 0

    lax.fori_loop(0, n * per, tile, 0)


def permute_kernel(held, pair, out, wide, flat):
    n, wp, cap = held.shape
    per = cap // LANES
    tiles = n * per
    for k in range(tiles):
        half = slice((k % per) * LANES, (k % per + 1) * LANES)
        flat[k : k + 1, :] = pair[k // per : k // per + 1, half]
        wide[k] = held[k // per, :, (k % per) * LANES : (k % per + 1) * LANES].astype(jnp.float32)

    def tile(block, half):
        p = flat[pl.ds(block * per + half, 1), :]
        where = jnp.broadcast_to(lax.shift_right_logical(p, 7), (8, LANES))
        lane = jnp.broadcast_to(lax.bitwise_and(p, LANES - 1), (8, LANES))
        parts = [jnp.zeros((8, LANES), jnp.float32) for _ in range(wp // 8)]
        for k in range(tiles):
            hit = where == k
            for r in range(wp // 8):
                got = jnp.take_along_axis(wide[k, r * 8 : (r + 1) * 8, :], lane, axis=1)
                parts[r] = jnp.where(hit, got, parts[r])
        whole = jnp.concatenate(parts, axis=0).astype(jnp.bfloat16)
        out[block, :, half * LANES : (half + 1) * LANES] = whole

    def both(block, _):
        for half in range(per):
            tile(block, half)
        return 0

    lax.fori_loop(0, n, both, 0)


def update_kernel(
    ids,
    meta,
    gaps,
    w,
    bias_in,
    bias_hid,
    freq,
    phase,
    self_all,
    part_all,
    own,
    memory,
    out,
    sems,
    out_sems,
    flat,
    rows,
    turned,
    gate_parts,
    gate_hid,
    equal,
    columns,
    fresh,
):
    c, n, wp, cap = self_all.shape
    node_rows = memory.shape[1]
    per = cap // LANES
    tiles = n * per
    g3 = 3 * wp
    groups = LANES // wp
    pieces = sems.shape[0]
    finish = load_rows(wp, node_rows, pieces, memory, flat, rows, sems)

    from_col = lax.broadcasted_iota(jnp.int32, (g3, g3), 0)
    to_col = lax.broadcasted_iota(jnp.int32, (g3, g3), 1)
    gate, feature = to_col // wp, lax.rem(to_col, wp)
    order = (from_col == 3 * feature + gate).astype(jnp.float32).astype(jnp.bfloat16)

    to_row = lax.broadcasted_iota(jnp.int32, (g3, g3), 0)
    hit = lax.broadcasted_iota(jnp.int32, (g3, g3), 1) == 3 * lax.rem(to_row, wp) + to_row // wp
    bias_x, bias_h = (
        jnp.sum(jnp.where(hit, ref[...], 0.0), axis=1, keepdims=True) for ref in (bias_in, bias_hid)
    )
    wide = (freq.shape[1],) * 2
    same_place = lax.broadcasted_iota(jnp.int32, wide, 0) == lax.broadcasted_iota(jnp.int32, wide, 1)
    rate, shift_by = (
        jnp.sum(jnp.where(same_place, ref[...], 0.0), axis=1, keepdims=True) for ref in (freq, phase)
    )

    def weights(kind):
        rows = w[:, kind].reshape(c * wp, g3)
        return jnp.dot(rows, order, preferred_element_type=jnp.float32).astype(jnp.bfloat16)

    w_self, w_part, w_time, w_hid = (weights(k) for k in range(4))
    over_in = (((0,), (0,)), ((), ()))

    def mm(a, b):
        return lax.dot_general(a, b, over_in, preferred_element_type=jnp.float32)

    gate_parts[2 * g3 :, :] = jnp.ones((gate_parts.shape[0] - 2 * g3, n * cap), jnp.bfloat16)

    def chunk(b, _):
        lanes = pl.ds(pl.multiple_of(b * cap, cap), cap)
        xs = self_all[:, b].reshape(c * wp, cap)
        xp = part_all[:, b].reshape(c * wp, cap)
        gap = jnp.concatenate([gaps[pl.ds(b * per + h, 1), :] for h in range(per)], axis=1)
        encoded = jnp.cos(gap * rate + shift_by).astype(jnp.bfloat16)
        gi = mm(w_self, xs) + mm(w_part, xp) + mm(w_time, encoded)
        gate_hid[:, lanes] = mm(w_hid, xs) + bias_h
        high = gi.astype(jnp.bfloat16)
        gate_parts[0:g3, lanes] = high
        gate_parts[g3 : 2 * g3, lanes] = (gi - high.astype(jnp.float32)).astype(jnp.bfloat16)
        return 0

    lax.fori_loop(0, n, chunk, 0)

    def column(i, _):
        lanes = pl.ds(pl.multiple_of(lax.rem(i, per) * LANES, LANES), LANES)
        row = jnp.broadcast_to(meta[i // per, 0:1, lanes].astype(jnp.float32), (LANES, LANES))
        columns[pl.ds(pl.multiple_of(i * LANES, LANES), LANES), :] = row.T
        return 0

    lax.fori_loop(0, tiles, column, 0)

    def means(b, _):
        lanes = pl.ds(pl.multiple_of(b * cap, cap), cap)
        for h in range(per):
            row = meta[b, 0:1, h * LANES : (h + 1) * LANES].astype(jnp.float32)
            same = (columns[...] == row).astype(jnp.float32).astype(jnp.bfloat16)
            equal[:, h * LANES : (h + 1) * LANES] = same
        sums = jnp.dot(gate_parts[...], equal[...], preferred_element_type=jnp.float32)
        mean = (sums[0:g3] + sums[g3 : 2 * g3]) / sums[2 * g3 : 2 * g3 + 1]
        gx = mean + bias_x
        gh = gate_hid[:, lanes]
        reset = jax.nn.sigmoid(gx[0:wp] + gh[0:wp])
        keep = jax.nn.sigmoid(gx[wp : 2 * wp] + gh[wp : 2 * wp])
        cand = jnp.tanh(gx[2 * wp :] + reset * gh[2 * wp :])
        fresh[:, lanes] = (1.0 - keep) * cand + keep * own[:, lanes]
        return 0

    lax.fori_loop(0, n, means, 0)
    finish()
    group_of = lax.broadcasted_iota(jnp.int32, (1, LANES), 1) // wp

    def tile(i, _):
        block, half = i // per, lax.rem(i, per)
        value = fresh[:, pl.ds(pl.multiple_of(i * LANES, LANES), LANES)]
        turned[...] = jnp.concatenate([value] * groups, axis=0).T

        def slot(j, _):
            node = ids[block, 0, half * LANES + j]
            safe = jnp.minimum(node, node_rows - 1)
            group = lax.bitwise_and(lax.shift_right_logical(safe, 7), groups - 1)
            group = jnp.where(node < node_rows, group, groups)
            pltpu.store(
                rows.at[pl.ds(row_of(safe, groups), 1), :],
                turned[pl.ds(j, 1), :],
                mask=group_of == group,
            )
            return 0

        lax.fori_loop(0, LANES, slot, 0, unroll=16)
        return 0

    lax.fori_loop(0, tiles, tile, 0)
    step = node_rows // pieces
    per_piece = step // (groups * LANES)

    def back(q, _):
        x = rows[pl.ds(pl.multiple_of(q * LANES, LANES), LANES), :].T
        for k in range(groups):
            lanes = pl.ds(pl.multiple_of((q * groups + k) * LANES, LANES), LANES)
            flat[:, lanes] = x[k * wp : (k + 1) * wp]
        return 0

    copies = []
    for i in range(pieces):
        lax.fori_loop(i * per_piece, (i + 1) * per_piece, back, 0, unroll=4)
        part = pl.ds(i * step, step)
        copies.append(pltpu.make_async_copy(flat.at[:, part], out.at[:, part], out_sems.at[i]))
        copies[-1].start()
    for copy in copies:
        copy.wait()


def comm(collective):
    return pltpu.CompilerParams(collective_id=collective, has_side_effects=True)


def dma(*shape):
    return pltpu.SemaphoreType.DMA(shape)


def local(
    n,
    c,
    memory,
    last_tick,
    slot_node,
    slot_pair,
    slot_tick,
    block_count,
    time_freq,
    time_phase,
    w_pair,
    w_time,
    w_hidden,
    bias_input,
    bias_hidden,
):
    wp, node_rows = memory.shape
    cap = slot_node.shape[1]
    total = n * cap
    tiles = total // LANES
    g3 = 3 * wp
    f32, i32, b16 = jnp.float32, jnp.int32, jnp.bfloat16
    shape = jax.ShapeDtypeStruct
    pieces = 8
    sent = (shape((n, 2, cap), i32), shape((c, 4, wp, g3), b16))
    meta, w = pl.pallas_call(
        lambda *refs: prepare_kernel(*refs, node_rows),
        out_shape=sent,
        in_specs=[VM, VM, SM, VM, VM, VM],
        out_specs=(VM, VM),
        name="prepare",
    )(slot_node, slot_tick, block_count, w_pair.reshape(wp, 2 * c * g3), w_time, w_hidden)
    meta, w = pl.pallas_call(
        functools.partial(first_kernel, n, c),
        out_shape=(shape(meta.shape, i32), shape(w.shape, b16)),
        in_specs=[VM, VM],
        out_specs=(VM, VM),
        scratch_shapes=[dma(n), dma(n), dma(c), dma(c)],
        compiler_params=comm(1),
        name="first",
    )(meta, w)
    own, own16, gaps = pl.pallas_call(
        gather_kernel,
        out_shape=(shape((wp, total), f32), shape((n, wp, cap), b16), shape((tiles, LANES), f32)),
        in_specs=[SM, VM, VM, ANY],
        out_specs=(VM, VM, VM),
        scratch_shapes=[
            pltpu.VMEM((wp, node_rows), f32),
            pltpu.VMEM((node_rows * wp // LANES, LANES), f32),
            pltpu.VMEM((LANES, LANES), f32),
            pltpu.VMEM((LANES, LANES), i32),
            dma(pieces),
        ],
        name="gather",
    )(meta, meta, last_tick.reshape(node_rows // LANES, LANES), memory)
    everyone = shape((c, n, wp, cap), b16)
    held, self_all = pl.pallas_call(
        functools.partial(reply_kernel, n, c),
        out_shape=(shape((n, wp, cap), b16), everyone),
        in_specs=[VM],
        out_specs=(VM, VM),
        scratch_shapes=[dma(n), dma(n)] + [dma(c, n)] * 4,
        compiler_params=comm(2),
        name="reply",
    )(own16)
    perm = pl.pallas_call(
        permute_kernel,
        out_shape=shape((n, wp, cap), b16),
        in_specs=[VM, VM],
        out_specs=VM,
        scratch_shapes=[pltpu.VMEM((tiles, wp, LANES), f32), pltpu.VMEM((tiles, LANES), i32)],
        name="permute",
    )(held, slot_pair)
    part_all = pl.pallas_call(
        functools.partial(spread_kernel, n, c),
        out_shape=everyone,
        in_specs=[VM],
        out_specs=VM,
        scratch_shapes=[dma(n), dma(n)] + [dma(c, n)] * 4,
        compiler_params=comm(3),
        name="spread",
    )(perm)
    extra = 16
    return pl.pallas_call(
        update_kernel,
        out_shape=shape((wp, node_rows), f32),
        in_specs=[SM] + [VM] * 10 + [ANY],
        out_specs=ANY,
        scratch_shapes=[
            dma(pieces),
            dma(pieces),
            pltpu.VMEM((wp, node_rows), f32),
            pltpu.VMEM((node_rows * wp // LANES, LANES), f32),
            pltpu.VMEM((LANES, LANES), f32),
            pltpu.VMEM((2 * g3 + extra, total), b16),
            pltpu.VMEM((g3, total), f32),
            pltpu.VMEM((total, cap), b16),
            pltpu.VMEM((total, LANES), f32),
            pltpu.VMEM((wp, total), f32),
        ],
        name="update",
    )(
        meta,
        meta,
        gaps,
        w,
        bias_input.reshape(1, g3),
        bias_hidden.reshape(1, g3),
        time_freq.reshape(1, -1),
        time_phase.reshape(1, -1),
        self_all,
        part_all,
        own,
        memory,
    )


def solution(mesh):
    placed = (
        P("cols", "rows"),
        P("rows"),
        P("rows", None),
        P("rows", None),
        P("rows", None),
        P("rows", None),
        P(),
        P(),
        P("cols", None, None),
        P("cols", None),
        P("cols", None),
        P("cols"),
        P("cols"),
    )
    return jax.shard_map(
        functools.partial(local, mesh.shape["rows"], mesh.shape["cols"]),
        mesh=mesh,
        in_specs=placed,
        out_specs=P("cols", "rows"),
        check_vma=False,
    )
```

profile of v0, /device:TPU:0, one launch (start us, length us, event | category | flops | bytes accessed | tf_op | source)
XLA Modules:
  0.0 97.2 jit_solution(14131656311918129214)
XLA Ops:
  0.0 1.4 %copy.14 = bf16[4,8,2,384]{3,1,2,0:T(8,128)(2,1)} copy(bf16[4,8,2,384]{3,2,1,0:T(2,128)(2,1)} %bitcast.9) | data formatting | bytes 98304
  1.4 1.6 %prepare.1 = (s32[8,2,256]{2,1,0:T(2,128)}, bf16[4,4,32,96]{3,2,1,0:T(8,128)(2,1)}) custom-call(s32[8,256]{1,0:T(8,128)} %refs_0_.1, s32[8,256]{1,0:T(8,128)} %refs_1_.1, s32[1,8]{1,0:T(1,128)} %refs_2_.1, bf16[32,768]{1,0:T(8,128)(2,1)} %bitcast.7, bf16[32,384]{1,0:T(8,128)(2,1)} %refs_4_.1, bf16[32,384]{1,0:T(8,128)(2,1)} %refs_5_.1), custom_call_target="tpu_custom_call" | custom-call | tf_op jit(solution)/shard_map/prepare/pallas_call | solution.py:467
  3.1 11.6 %first.1 = (s32[8,2,256]{2,1,0:T(2,128)}, bf16[4,4,32,96]{3,2,1,0:T(8,128)(2,1)}) custom-call(s32[8,2,256]{2,1,0:T(2,128)} %get-tuple-element.14.meta, bf16[4,4,32,96]{3,2,1,0:T(8,128)(2,1)} %get-tuple-element.15.w), custom_call_target="tpu_custom_call" | custom-call | tf_op jit(solution)/shard_map/first/pallas_call | solution.py:474
  14.6 16.6 %gather.1 = (f32[32,2048]{1,0:T(8,128)}, bf16[8,32,256]{2,1,0:T(8,128)(2,1)}, f32[16,128]{1,0:T(8,128)}) custom-call(s32[8,2,256]{2,1,0:T(2,128)} %get-tuple-element.16.ids.meta, s32[8,2,256]{2,1,0:T(2,128)} %get-tuple-element.16.ids.meta, s32[256,128]{1,0:T(8,128)} %bitcast.8, f32[32,32768]{1,0:T(8,128)} %memory.3), custom_call_target="tpu_custom_call" | custom-call | tf_op jit(solution)/shard_map/gather/pallas_call | solution.py:483
  31.3 15.7 %reply.1 = (bf16[8,32,256]{2,1,0:T(8,128)(2,1)}, bf16[4,8,32,256]{3,2,1,0:T(8,128)(2,1)}) custom-call(bf16[8,32,256]{2,1,0:T(8,128)(2,1)} %get-tuple-element.19.src), custom_call_target="tpu_custom_call" | custom-call | tf_op jit(solution)/shard_map/reply/pallas_call | solution.py:498
  47.1 2.8 %permute.1.perm = bf16[8,32,256]{2,1,0:T(8,128)(2,1)} custom-call(bf16[8,32,256]{2,1,0:T(8,128)(2,1)} %get-tuple-element.21.held, s32[8,256]{1,0:T(8,128)} %pair.1), custom_call_target="tpu_custom_call" | custom-call | tf_op jit(solution)/shard_map/permute/pallas_call | solution.py:507
  49.8 17.4 %spread.1.part_all = bf16[4,8,32,256]{3,2,1,0:T(8,128)(2,1)} custom-call(bf16[8,32,256]{2,1,0:T(8,128)(2,1)} %permute.1.perm), custom_call_target="tpu_custom_call" | custom-call | tf_op jit(solution)/shard_map/spread/pallas_call | solution.py:515
  67.2 30.0 %update.1 = f32[32,32768]{1,0:T(8,128)} custom-call(s32[8,2,256]{2,1,0:T(2,128)} %get-tuple-element.16.ids.meta, s32[8,2,256]{2,1,0:T(2,128)} %get-tuple-element.16.ids.meta, f32[16,128]{1,0:T(8,128)} %get-tuple-element.17.gaps, bf16[4,4,32,96]{3,2,1,0:T(8,128)(2,1)} %get-tuple-element.18.w, f32[1,96]{1,0:T(1,128)} %bitcast.10, f32[1,96]{1,0:T(1,128)} %bitcast.11, ...), custom_call_target="tpu_custom_call" | custom-call | tf_op jit(solution)/shard_map/update/pallas_call | solution.py:525
where the time goes:
time: 97.6 us; the launch traced here: 97.2 us
  Pallas kernels  95.8 us (98%)
  local copies, waits for them, and re-layouts  1.41 us (1%)
    pallas_call x1, Pallas kernels, local(): pl.pallas_call(update_kernel, out_shape=shape((wp, node_rows), f32), in_s...  30 us
    pallas_call x1, Pallas kernels, local(): pl.pallas_call(functools.partial(spread_kernel, n, c), out_shape=everyone...  17.4 us
    pallas_call x1, Pallas kernels, local(): pl.pallas_call(gather_kernel, out_shape=(shape((wp, total), f32), shape((...  16.6 us
    pallas_call x1, Pallas kernels, local(): pl.pallas_call(functools.partial(reply_kernel, n, c), out_shape=(shape((n...  15.7 us
    pallas_call x1, Pallas kernels, local(): pl.pallas_call(functools.partial(first_kernel, n, c), out_shape=(shape(me...  11.6 us
    pallas_call x1, Pallas kernels, local(): pl.pallas_call(permute_kernel, out_shape=shape((n, wp, cap), b16), in_spe...  2.75 us

commit v1 on v0

v1 whole, which is shorter than its diff:
```python
import functools

import jax
import jax.numpy as jnp
from jax import lax
from jax.experimental import pallas as pl
from jax.experimental.pallas import tpu as pltpu
from jax.sharding import PartitionSpec as P

MESH = pl.DeviceIdType.MESH
LANES = 128
SHIFT = 16
VM = pl.BlockSpec(memory_space=pltpu.VMEM)
SM = pl.BlockSpec(memory_space=pltpu.SMEM)
ANY = pl.BlockSpec(memory_space=pl.ANY)
PIECES = 8
F32, I32, B16 = jnp.float32, jnp.int32, jnp.bfloat16


def mate(me, k, n, back=False):
    if n & (n - 1):
        return lax.rem(me + (n - k if back else k), n)
    out = me
    for i in range(n.bit_length() - 1):
        if k >> i & 1:
            out = out + (1 << i) * (1 - 2 * lax.rem(lax.div(me, 1 << i), 2))
    return out


def remote(src, dst, send, recv, axis, peer):
    return pltpu.make_async_remote_copy(
        src_ref=src,
        dst_ref=dst,
        send_sem=send,
        recv_sem=recv,
        device_id={axis: peer},
        device_id_type=MESH,
    )


def chain(c, block, first, places, sems):
    col = lax.axis_index("cols")
    n = len(places)
    ways = (True, False)

    def hop(source, t, k, right):
        send, recv = sems[0:2] if right else sems[2:4]
        ref = block(source, places[k])
        return remote(
            first(k) if t == 0 else ref,
            ref,
            send.at[t, k],
            recv.at[t, k],
            "cols",
            col + 1 if right else col - 1,
        )

    def goes(right):
        return col < c - 1 if right else col > 0

    def where_from(t, right):
        source = col - t if right else col + t
        there = source >= 0 if right else source < c
        return source, there

    def begin(k):
        for right in ways:

            @pl.when(goes(right))
            def _(right=right):
                hop(col, 0, k, right).start()

    def rest(done):
        for t in range(1, c):
            for k in range(n):
                for right in ways:
                    source, there = where_from(t, right)

                    @pl.when(there)
                    def _(right=right, source=source, t=t, k=k):
                        hop(source, t - 1, k, right).wait_recv()

                    @pl.when(jnp.logical_and(there, goes(right)))
                    def _(right=right, source=source, t=t, k=k):
                        hop(source, t, k, right).start()

                if t == c - 1:
                    done(k)

        for t in range(c - 1):
            for right in ways:
                source, there = where_from(t, right)

                @pl.when(jnp.logical_and(there, goes(right)))
                def _(right=right, source=source, t=t):
                    for k in range(n):
                        hop(source, t, k, right).wait_send()

    return begin, rest


def lanes_of(i, width):
    return pl.ds(pl.multiple_of(i * width, width), width)


def spread_row(ref, hit):
    return jnp.sum(jnp.where(hit, ref[...], 0.0), axis=1, keepdims=True)


def over_in(a, b):
    return lax.dot_general(a, b, (((0,), (0,)), ((), ())), preferred_element_type=F32)


def iota(shape, axis):
    return lax.broadcasted_iota(I32, shape, axis)


def main_kernel(
    n,
    c,
    nodes,
    ticks,
    counts,
    pair,
    last,
    w_pair,
    w_time,
    w_hid,
    bias_in,
    bias_hid,
    freq,
    phase,
    memory,
    meta,
    fresh,
    rows_out,
    flat,
    rows,
    ids,
    meta_src,
    w_src,
    w,
    picked,
    own,
    held,
    wide,
    where,
    perm,
    self_all,
    part_all,
    gaps,
    columns,
    equal,
    inverse,
    timed,
    pre,
    acc,
    load_sem,
    save_sem,
    id_sem,
    meta_s,
    meta_r,
    w_s,
    w_r,
    reply_s,
    reply_r,
    self_s,
    self_r,
    spread_s,
    spread_r,
    *hops,
):
    row, col = lax.axis_index("rows"), lax.axis_index("cols")
    cap = nodes.shape[1]
    wp, node_rows = memory.shape
    groups = LANES // wp
    rows_n = node_rows // groups
    g3 = 3 * wp
    per = cap // LANES
    tiles = n * per
    width = c * g3

    barrier = pltpu.get_barrier_semaphore()
    for axis, size, me in (("rows", n, row), ("cols", c, col)):
        for k in range(1, size):
            pl.semaphore_signal(
                barrier, inc=1, device_id={axis: mate(me, k, size)}, device_id_type=MESH
            )

    step = rows_n // PIECES
    loads = []
    for i in range(PIECES):
        for k in range(groups):
            part = pl.ds(k * rows_n + i * step, step)
            loads.append(pltpu.make_async_copy(memory.at[:, part], flat.at[:, part], load_sem.at[i, k]))
    for copy in loads:
        copy.start()

    lane = iota((1, cap), 1)
    for b in range(n):
        mine = nodes[b : b + 1, :] - b * node_rows
        group = jnp.zeros((1, cap), I32)
        for k in range(1, groups):
            group = group + jnp.where(mine >= k * rows_n, 1, 0)
        code = mine + group * ((1 << SHIFT) - rows_n)
        meta_src[b, 0:1, :] = jnp.where(lane < counts[0, b], code, rows_n)
        meta_src[b, 1:2, :] = ticks[b : b + 1, :]

    pl.semaphore_wait(barrier, n + c - 2)
    metas = [
        remote(
            meta_src.at[mate(row, k, n)],
            meta.at[row],
            meta_s.at[k],
            meta_r.at[k],
            "rows",
            mate(row, k, n),
        )
        for k in range(1, n)
    ]
    for copy in reversed(metas):
        copy.start()
    meta[row] = meta_src[row]

    q = iota((1, LANES), 1)
    gate = jnp.zeros((1, LANES), I32)
    for k in range(1, 4):
        gate = gate + jnp.where(q >= k * wp, 1, 0)
    target = jnp.where(q < g3, 3 * (q - gate * wp) + gate, -width)
    stacked = jnp.concatenate([w_pair[:, 0, :], w_pair[:, 1, :], w_time[...], w_hid[...]], axis=0)
    from_col = iota((width, LANES), 0)
    for p in range(c):
        pick = jnp.where(from_col == target + p * g3, 1.0, 0.0).astype(B16)
        block = jnp.dot(stacked, pick, preferred_element_type=F32).astype(B16)
        for k in range(4):
            w_src[p, k] = block[k * wp : (k + 1) * wp]
    sends = [
        remote(
            w_src.at[mate(col, k, c)], w.at[col], w_s.at[k], w_r.at[k], "cols", mate(col, k, c)
        )
        for k in range(1, c)
    ]
    for copy in sends:
        copy.start()
    w[col] = w_src[col]

    rows[rows_n:, :] = jnp.zeros((8, LANES), F32)
    per_piece = step // LANES

    def turn(i, _):
        block = [flat[:, lanes_of(k * (rows_n // LANES) + i, LANES)] for k in range(groups)]
        rows[lanes_of(i, LANES), :] = jnp.concatenate(block, 0).T
        return 0

    saves = []
    for i in range(PIECES):
        for k in range(groups):
            loads[i * groups + k].wait()
        lax.fori_loop(i * per_piece, (i + 1) * per_piece, turn, 0, unroll=8)
        part = pl.ds(i * step, step)
        saves.append(pltpu.make_async_copy(rows.at[part], rows_out.at[part], save_sem.at[i]))
        saves[-1].start()

    sources = [mate(row, k, n, True) for k in range(n)]
    others = [mate(row, k, n) for k in range(n)]
    id_copies = [
        pltpu.make_async_copy(meta.at[sources[k]], ids.at[sources[k]], id_sem.at[k])
        for k in range(n)
    ]

    def arrive(k):
        if k:
            remote(
                meta_src.at[others[k]],
                meta.at[sources[k]],
                meta_s.at[k],
                meta_r.at[k],
                "rows",
                others[k],
            ).wait_recv()
        id_copies[k].start()

    def reply(k):
        b = sources[k]
        return remote(
            self_all.at[col, b], held.at[row], reply_s.at[k], reply_r.at[k], "rows", b
        )

    def reply_in(k):
        return remote(
            self_all.at[col, others[k]],
            held.at[others[k]],
            reply_s.at[k],
            reply_r.at[k],
            "rows",
            others[k],
        )

    def self_out(k, j):
        ref = self_all.at[col, sources[k]]
        return remote(ref, ref, self_s.at[j, k], self_r.at[j, k], "cols", mate(col, j, c))

    def self_in(k, j):
        ref = self_all.at[mate(col, j, c, True), sources[k]]
        return remote(ref, ref, self_s.at[j, k], self_r.at[j, k], "cols", mate(col, j, c))

    def gather(b):
        def slot(j, _):
            for u in range(32):
                r = lax.bitwise_and(ids[b, 0, j * 32 + u], (1 << SHIFT) - 1)
                picked[pl.ds(j * 32 + u, 1), :] = rows[pl.ds(r, 1), :]
            return 0

        lax.fori_loop(0, cap // 32, slot, 0)
        for half in range(per):
            lanes = slice(half * LANES, (half + 1) * LANES)
            group = lax.shift_right_logical(meta[b, 0:1, lanes], SHIFT)
            turned = picked[lanes, :].T
            mine = turned[0:wp]
            for k in range(1, groups):
                mine = jnp.where(group == k, turned[k * wp : (k + 1) * wp], mine)
            own[:, lanes_of(b * per + half, LANES)] = mine
            self_all[col, b, :, lanes] = mine.astype(B16)

    arrive(0)
    for k in range(n):
        if k + 1 < n:
            arrive(k + 1)
        id_copies[k].wait()
        gather(sources[k])
        if k:
            reply(k).start()
        else:
            held[row] = self_all[col, row]
        for j in reversed(range(1, c)):
            self_out(k, j).start()

    low, high = [], []
    hi_rows = node_rows // LANES
    old = last[...]
    table = jnp.concatenate(
        [lax.shift_right_logical(old, 8).astype(F32), lax.bitwise_and(old, 255).astype(F32)], axis=1
    ).astype(B16)
    hi_iota = iota((hi_rows, cap), 0)
    lo_iota = iota((LANES, cap), 0)

    def gap_of(b, _):
        code = meta[b, 0:1, :]
        r = lax.bitwise_and(code, (1 << SHIFT) - 1)
        hi = lax.shift_right_logical(r, 7) + lax.shift_right_logical(code, SHIFT) * (rows_n // LANES)
        pick = jnp.where(hi_iota == hi, 1.0, 0.0).astype(B16)
        found = over_in(table, pick)
        found = found[0:LANES] * 256.0 + found[LANES:]
        found = jnp.where(lo_iota == lax.bitwise_and(r, LANES - 1), found, 0.0)
        gaps[b] = meta[b, 1:2, :].astype(F32) - jnp.sum(found, axis=0, keepdims=True)
        return 0

    lax.fori_loop(0, n, gap_of, 0)

    for k in range(tiles):
        half = slice((k % per) * LANES, (k % per + 1) * LANES)
        where[k : k + 1, :] = pair[k // per : k // per + 1, half]

    def column(i, _):
        block, half = lax.div(i, per), lax.rem(i, per)
        code = meta[block, 0:1, lanes_of(half, LANES)].astype(F32)
        columns[lanes_of(i, LANES), :] = jnp.broadcast_to(code, (LANES, LANES)).T
        return 0

    lax.fori_loop(0, tiles, column, 0, unroll=4)

    for k in range(1, n):
        reply_in(k).wait_recv()

    for k in range(tiles):
        wide[k] = held[k // per, :, (k % per) * LANES : (k % per + 1) * LANES].astype(F32)

    def permute(block, _):
        for half in range(per):
            p = where[pl.ds(block * per + half, 1), :]
            tile = jnp.broadcast_to(lax.shift_right_logical(p, 7), (8, LANES))
            place = jnp.broadcast_to(lax.bitwise_and(p, LANES - 1), (8, LANES))
            parts = [jnp.zeros((8, LANES), F32) for _ in range(wp // 8)]
            for k in range(tiles):
                hit = tile == k
                for r in range(wp // 8):
                    got = jnp.take_along_axis(wide[k, r * 8 : (r + 1) * 8, :], place, axis=1)
                    parts[r] = jnp.where(hit, got, parts[r])
            whole = jnp.concatenate(parts, axis=0).astype(B16)
            perm[block, :, half * LANES : (half + 1) * LANES] = whole
        return 0

    lax.fori_loop(0, n, permute, 0)

    spreads = [
        remote(
            perm.at[others[k]],
            part_all.at[col, row],
            spread_s.at[k],
            spread_r.at[k],
            "rows",
            others[k],
        )
        for k in range(1, n)
    ]
    for copy in spreads:
        copy.start()

    def spread_in(k):
        return remote(
            perm.at[others[k]],
            part_all.at[col, sources[k]],
            spread_s.at[k],
            spread_r.at[k],
            "rows",
            others[k],
        )

    begin, rest = chain(
        c,
        lambda source, place: part_all.at[source, place],
        lambda k: part_all.at[col, sources[k]] if k else perm.at[row],
        sources,
        hops,
    )
    begin(0)
    part_all[col, row] = perm[row]

    def same_of(i, _):
        block, half = lax.div(i, per), lax.rem(i, per)
        code = meta[block, 0:1, lanes_of(half, LANES)].astype(F32)
        same = jnp.where(columns[...] == code, 1.0, 0.0)
        equal[:, lanes_of(i, LANES)] = same.astype(B16)
        inverse[:, lanes_of(i, LANES)] = 1.0 / jnp.sum(same, axis=0, keepdims=True)
        return 0

    lax.fori_loop(0, tiles, same_of, 0)
    for k in range(1, n):
        spread_in(k).wait_recv()
        begin(k)

    for k in range(1, c):
        remote(
            w_src.at[mate(col, k, c)],
            w.at[mate(col, k, c, True)],
            w_s.at[k],
            w_r.at[k],
            "cols",
            mate(col, k, c),
        ).wait_recv()
    w_self, w_part, w_time_all, w_hid_all = (
        w[:, k].reshape(c * wp, LANES)[:, 0:g3] for k in range(4)
    )
    to_row = iota((g3, g3), 0)
    to_gate = jnp.zeros((g3, g3), I32)
    for k in range(1, 3):
        to_gate = to_gate + jnp.where(to_row >= k * wp, 1, 0)
    hit = iota((g3, g3), 1) == 3 * (to_row - to_gate * wp) + to_gate
    bias_x, bias_h = spread_row(bias_in, hit), spread_row(bias_hid, hit)
    square = (freq.shape[1],) * 2
    diagonal = iota(square, 0) == iota(square, 1)
    rate, shift_by = spread_row(freq, diagonal), spread_row(phase, diagonal)
    acc[...] = jnp.zeros(acc.shape, F32)

    def time_part(b, _):
        encoded = jnp.cos(gaps[b] * rate + shift_by).astype(B16)
        timed[:, lanes_of(b, cap)] = over_in(w_time_all, encoded)
        return 0

    lax.fori_loop(0, n, time_part, 0)

    for k in range(n):
        for j in range(1, c):
            self_in(k, j).wait_recv()

    def self_part(b, _):
        lanes = lanes_of(b, cap)
        xs = self_all[:, b].reshape(c * wp, cap)
        gx = over_in(w_self, xs) + bias_x
        gh = over_in(w_hid_all, xs) + bias_h
        pre[0 : 2 * wp, lanes] = gx[0 : 2 * wp] + gh[0 : 2 * wp]
        pre[2 * wp : 3 * wp, lanes] = gx[2 * wp :]
        pre[3 * wp :, lanes] = gh[2 * wp :]
        return 0

    lax.fori_loop(0, n, self_part, 0)

    def add_block(k):
        b = sources[k]
        xp = part_all[:, b].reshape(c * wp, cap)
        gi = over_in(w_part, xp) + timed[:, lanes_of(b, cap)]
        big = gi.astype(B16)
        both = jnp.concatenate([big, (gi - big.astype(F32)).astype(B16)], axis=0)
        mine = pl.ds(pl.multiple_of(b * cap, cap), cap)

        def into(i, _):
            lanes = lanes_of(i, cap)
            sums = jnp.dot(both, equal[mine, lanes], preferred_element_type=F32)
            acc[:, lanes] += sums[0:g3] + sums[g3:]
            return 0

        lax.fori_loop(0, n, into, 0)

    rest(add_block)

    def gates(b, _):
        lanes = lanes_of(b, cap)
        mean = acc[:, lanes] * inverse[:, lanes]
        rz = jax.nn.sigmoid(mean[0 : 2 * wp] + pre[0 : 2 * wp, lanes])
        reset, keep = rz[0:wp], rz[wp:]
        cand = jnp.tanh(mean[2 * wp :] + pre[2 * wp : 3 * wp, lanes] + reset * pre[3 * wp :, lanes])
        fresh[:, lanes] = (1.0 - keep) * cand + keep * own[:, lanes]
        return 0

    lax.fori_loop(0, n, gates, 0)

    for copy in saves:
        copy.wait()
    for copy in metas + sends + spreads:
        copy.wait_send()
    for k in range(n):
        if k:
            reply(k).wait_send()
        for j in range(1, c):
            self_out(k, j).wait_send()


def scatter_kernel(ids, fresh, rows_in, out, flat, rows, turned, load_sem, out_sem):
    n, _, cap = ids.shape
    wp, node_rows = out.shape
    groups = LANES // wp
    rows_n = node_rows // groups
    tiles = n * cap // LANES
    step = rows_n // PIECES
    loads = [
        pltpu.make_async_copy(
            rows_in.at[pl.ds(i * step, step)], rows.at[pl.ds(i * step, step)], load_sem.at[i]
        )
        for i in range(PIECES)
    ]
    for copy in loads:
        copy.start()

    def tile(i, _):
        value = fresh[:, lanes_of(i, LANES)]
        turned[lanes_of(i, LANES), :] = jnp.concatenate([value] * groups, axis=0).T
        return 0

    lax.fori_loop(0, tiles, tile, 0, unroll=4)
    for copy in loads:
        copy.wait()
    group_of = lax.div(iota((1, LANES), 1), wp)

    def slots(b, _):
        def slot(j, _):
            for u in range(32):
                code = ids[b, 0, j * 32 + u]
                r = lax.bitwise_and(code, (1 << SHIFT) - 1)
                pltpu.store(
                    rows.at[pl.ds(r, 1), :],
                    turned[pl.ds(b * cap + j * 32 + u, 1), :],
                    mask=group_of == lax.shift_right_logical(code, SHIFT),
                )
            return 0

        lax.fori_loop(0, cap // 32, slot, 0)
        return 0

    lax.fori_loop(0, n, slots, 0)
    per_piece = step // LANES

    def back(i, _):
        x = rows[lanes_of(i, LANES), :].T
        for k in range(groups):
            flat[:, lanes_of(k * (rows_n // LANES) + i, LANES)] = x[k * wp : (k + 1) * wp]
        return 0

    copies = []
    for i in range(PIECES):
        lax.fori_loop(i * per_piece, (i + 1) * per_piece, back, 0, unroll=8)
        for k in range(groups):
            part = pl.ds(k * rows_n + i * step, step)
            copies.append(pltpu.make_async_copy(flat.at[:, part], out.at[:, part], out_sem.at[i, k]))
            copies[-1].start()
    for copy in copies:
        copy.wait()


def dma(*shape):
    return pltpu.SemaphoreType.DMA(shape)


def local(
    n,
    c,
    memory,
    last_tick,
    slot_node,
    slot_pair,
    slot_tick,
    block_count,
    time_freq,
    time_phase,
    w_pair,
    w_time,
    w_hidden,
    bias_input,
    bias_hidden,
):
    wp, node_rows = memory.shape
    cap = slot_node.shape[1]
    total = n * cap
    tiles = total // LANES
    g3 = 3 * wp
    groups = LANES // wp
    rows_n = node_rows // groups
    shape = jax.ShapeDtypeStruct
    vm = pltpu.VMEM
    meta, fresh, rows = pl.pallas_call(
        functools.partial(main_kernel, n, c),
        out_shape=(
            shape((n, 2, cap), I32),
            shape((wp, total), F32),
            shape((rows_n, LANES), F32),
        ),
        in_specs=[VM, VM, SM] + [VM] * 9 + [ANY],
        out_specs=(VM, VM, ANY),
        scratch_shapes=[
            vm((wp, node_rows), F32),
            vm((rows_n + 8, LANES), F32),
            pltpu.SMEM((n, 2, cap), I32),
            vm((n, 2, cap), I32),
            vm((c, 4, wp, LANES), B16),
            vm((c, 4, wp, LANES), B16),
            vm((cap, LANES), F32),
            vm((wp, total), F32),
            vm((n, wp, cap), B16),
            vm((tiles, wp, LANES), F32),
            vm((tiles, LANES), I32),
            vm((n, wp, cap), B16),
            vm((c, n, wp, cap), B16),
            vm((c, n, wp, cap), B16),
            vm((n, 1, cap), F32),
            vm((total, LANES), F32),
            vm((total, total), B16),
            vm((1, total), F32),
            vm((g3, total), F32),
            vm((4 * wp, total), F32),
            vm((g3, total), F32),
            dma(PIECES, groups),
            dma(PIECES),
            dma(n),
            dma(n),
            dma(n),
            dma(c),
            dma(c),
            dma(n),
            dma(n),
            dma(c, n),
            dma(c, n),
            dma(n),
            dma(n),
        ]
        + [dma(c, n)] * 4,
        compiler_params=pltpu.CompilerParams(collective_id=1, has_side_effects=True),
        name="exchange",
    )(
        slot_node,
        slot_tick,
        block_count,
        slot_pair,
        last_tick.reshape(node_rows // LANES, LANES),
        w_pair,
        w_time,
        w_hidden,
        bias_input.reshape(1, g3),
        bias_hidden.reshape(1, g3),
        time_freq.reshape(1, -1),
        time_phase.reshape(1, -1),
        memory,
    )
    return pl.pallas_call(
        scatter_kernel,
        out_shape=shape((wp, node_rows), F32),
        in_specs=[SM, VM, ANY],
        out_specs=ANY,
        scratch_shapes=[
            vm((wp, node_rows), F32),
            vm((rows_n + 8, LANES), F32),
            vm((total, LANES), F32),
            dma(PIECES),
            dma(PIECES, groups),
        ],
        name="scatter",
    )(meta, fresh, rows)


def solution(mesh):
    placed = (
        P("cols", "rows"),
        P("rows"),
        P("rows", None),
        P("rows", None),
        P("rows", None),
        P("rows", None),
        P(),
        P(),
        P("cols", None, None),
        P("cols", None),
        P("cols", None),
        P("cols"),
        P("cols"),
    )
    return jax.shard_map(
        functools.partial(local, mesh.shape["rows"], mesh.shape["cols"]),
        mesh=mesh,
        in_specs=placed,
        out_specs=P("cols", "rows"),
        check_vma=False,
    )
```

time: 97.6 us -> 64.6 us (0.66)
  Pallas kernels: 95.8 us -> 64.3 us
  local copies, waits for them, and re-layouts: 1.41 us -> 0 us
    pallas_call x7 -> x2, Pallas kernels: 95.8 us -> 64.3 us  [the longest x1 52.9 us: local(): pl.pallas_call(functools.partial(main_kernel, n, c), out_shape=(shape((n,...]
    unnamed x1 -> x0, local copies, waits for them, and re-layouts: 1.41 us -> none
where the time goes in v1:
time: 64.6 us; the launch traced here: 64.3 us
  Pallas kernels  64.3 us (100%)
    pallas_call x1, Pallas kernels, local(): pl.pallas_call(functools.partial(main_kernel, n, c), out_shape=(shape((n,...  52.9 us
    pallas_call x1, Pallas kernels, local(): pl.pallas_call(scatter_kernel, out_shape=shape((wp, node_rows), F32), in_...  11.4 us

profile of v1, /device:TPU:0, one launch (start us, length us, event | category | flops | bytes accessed | tf_op | source)
XLA Modules:
  0.0 64.3 jit_solution(6243436970392491866)
XLA Ops:
  0.0 52.9 %exchange.1 = (s32[8,2,256]{2,1,0:T(2,128)}, f32[32,2048]{1,0:T(8,128)}, f32[8192,128]{1,0:T(8,128)}) custom-call(s32[8,256]{1,0:T(8,128)} %nodes.1, s32[8,256]{1,0:T(8,128)} %ticks.1, s32[1,8]{1,0:T(1,128)} %counts.1, s32[8,256]{1,0:T(8,128)} %pair.1, s32[256,128]{1,0:T(8,128)} %bitcast.5, bf16[32,2,384]{2,1,0:T(2,128)(2,1)} %w_pair.1, ...), custom_call_target="tpu_custom_call" | custom-call | tf_op jit(solution)/shard_map/exchange/pallas_call | solution.py:619
  52.9 11.4 %scatter.1 = f32[32,32768]{1,0:T(8,128)} custom-call(s32[8,2,256]{2,1,0:T(2,128)} %get-tuple-element.8.ids, f32[32,2048]{1,0:T(8,128)} %get-tuple-element.9.fresh, f32[8192,128]{1,0:T(8,128)} %get-tuple-element.10.rows_in), custom_call_target="tpu_custom_call" | custom-call | tf_op jit(solution)/shard_map/scatter/pallas_call | solution.py:682

commit v2 on v1

v2 whole, which is shorter than its diff:
```python
import functools

import jax
import jax.numpy as jnp
from jax import lax
from jax.experimental import pallas as pl
from jax.experimental.pallas import tpu as pltpu
from jax.sharding import PartitionSpec as P

MESH = pl.DeviceIdType.MESH
LANES = 128
SHIFT = 16
VM = pl.BlockSpec(memory_space=pltpu.VMEM)
SM = pl.BlockSpec(memory_space=pltpu.SMEM)
ANY = pl.BlockSpec(memory_space=pl.ANY)
HBM = pl.BlockSpec(memory_space=pltpu.HBM)
PIECES = 4
VMEM_BYTES = 67_043_328
SELF_PARTS = 2
F32, I32, B16 = jnp.float32, jnp.int32, jnp.bfloat16


def mate(me, k, n, back=False):
    if n & (n - 1):
        return lax.rem(me + (n - k if back else k), n)
    out = me
    for i in range(n.bit_length() - 1):
        if k >> i & 1:
            out = out + (1 << i) * (1 - 2 * lax.rem(lax.div(me, 1 << i), 2))
    return out


def remote(src, dst, send, recv, axis, peer):
    return pltpu.make_async_remote_copy(
        src_ref=src,
        dst_ref=dst,
        send_sem=send,
        recv_sem=recv,
        device_id={axis: peer},
        device_id_type=MESH,
    )


def ladder(c, buffer, first, places, parts, sends, recvs):
    col = lax.axis_index("cols")
    ways = (True, False)
    n = len(places)
    each = n // parts

    def towards(steps, right):
        return col + steps if right else col - steps

    def has(d, right):
        return towards(-d, right) >= 0 if right else towards(-d, right) < c

    def fits(d, right):
        return towards(d, right) < c if right else towards(d, right) >= 0

    def send_sem(d, right):
        return sends.at[2 * d + right]

    def hop(d, k, right, stride):
        source = towards(stride - d, right)
        ref = buffer.at[source, places[k]]
        return remote(
            first(k) if d == stride else ref,
            ref,
            send_sem(d, right),
            recvs.at[source, k // each],
            "cols",
            towards(stride, right),
        )

    def landed(d, part, right):
        source = towards(-d, right)
        peer = jnp.minimum(col + 1, c - 1) if right else jnp.maximum(col - 1, 0)
        ref = buffer.at[source, pl.ds(0, each)]
        return remote(ref, ref, send_sem(d, right), recvs.at[source, part], "cols", peer)

    def when(*tests):
        return pl.when(functools.reduce(jnp.logical_and, tests))

    def begin(k):
        for d in (2, 1):
            for right in ways:
                if d < c:

                    @when(fits(d, right))
                    def _(d=d, right=right):
                        hop(d, k, right, d).start()

    def forward(part):
        for d in range(2, c - 1):
            for right in ways:

                @when(has(d, right), fits(1, right))
                def _(d=d, right=right):
                    landed(d, part, right).wait_recv()
                    for k in range(part * each, (part + 1) * each):
                        hop(d + 1, k, right, 1).start()

    def finish(part):
        for d in range(1, c):
            for right in ways:
                tests = [has(d, right)]
                if d > 1:
                    tests.append(jnp.logical_not(fits(1, right)))

                @when(*tests)
                def _(d=d, right=right):
                    landed(d, part, right).wait_recv()

    def drain():
        for right in ways:
            peer = jnp.minimum(col + 1, c - 1) if right else jnp.maximum(col - 1, 0)
            for d in range(1, c):
                if d < 3:
                    tests = [fits(d, right)]
                else:
                    tests = [has(d - 1, right), fits(1, right)]

                @when(*tests)
                def _(d=d, right=right, peer=peer):
                    ref = buffer.at[0]
                    remote(ref, ref, send_sem(d, right), recvs.at[0, 0], "cols", peer).wait_send()

    return begin, forward, finish, drain


def lanes_of(i, width):
    return pl.ds(pl.multiple_of(i * width, width), width)


def spread_row(ref, hit):
    return jnp.sum(jnp.where(hit, ref[...], 0.0), axis=1, keepdims=True)


def over_in(a, b):
    return lax.dot_general(a, b, (((0,), (0,)), ((), ())), preferred_element_type=F32)


def iota(shape, axis):
    return lax.broadcasted_iota(I32, shape, axis)


def main_kernel(n, c, *refs):
    given, memory, refs = refs[0:12], refs[12], refs[13:]
    meta, fresh, rows, refs = *refs[0:3], refs[3:]
    taken, in_sem, refs = refs[0:12], refs[12], refs[13:]
    fetches = [
        pltpu.make_async_copy(a, b, in_sem.at[i]) for i, (a, b) in enumerate(zip(given, taken))
    ]
    main_body(n, c, fetches, *taken, memory, meta, fresh, rows, *refs)


def main_body(
    n,
    c,
    fetches,
    nodes,
    ticks,
    counts,
    pair,
    last,
    w_pair,
    w_time,
    w_hid,
    bias_in,
    bias_hid,
    freq,
    phase,
    memory,
    meta,
    fresh,
    rows,
    flat,
    ids,
    meta_src,
    w_src,
    w,
    picked,
    own,
    held,
    wide,
    where,
    perm,
    self_all,
    part_all,
    gaps,
    columns,
    equal,
    number,
    timed,
    pre,
    acc,
    load_sem,
    id_sem,
    meta_s,
    meta_r,
    w_s,
    w_r,
    reply_s,
    reply_r,
    spread_s,
    spread_r,
    *hops,
):
    row, col = lax.axis_index("rows"), lax.axis_index("cols")
    cap = nodes.shape[1]
    wp, node_rows = memory.shape
    groups = LANES // wp
    rows_n = node_rows // groups
    g3 = 3 * wp
    per = cap // LANES
    tiles = n * per
    width = c * g3

    def group_row(b, half):
        return lax.shift_right_logical(meta[b, pl.ds(per + half, 1), :], SHIFT)

    def node_row(b, half):
        return meta[b, pl.ds(half, 1), :] + group_row(b, half) * rows_n

    def wide_row(row_of, b):
        return jnp.concatenate([row_of(b, half) for half in range(per)], axis=1)

    barrier = pltpu.get_barrier_semaphore()
    for axis, size, me in (("rows", n, row), ("cols", c, col)):
        for k in range(1, size):
            pl.semaphore_signal(
                barrier, inc=1, device_id={axis: mate(me, k, size)}, device_id_type=MESH
            )

    for copy in fetches:
        copy.start()
    step = rows_n // PIECES
    loads = []
    for i in range(PIECES):
        for k in range(groups):
            part = pl.ds(k * rows_n + i * step, step)
            loads.append(pltpu.make_async_copy(memory.at[:, part], flat.at[:, part], load_sem.at[i]))
    for copy in loads:
        copy.start()

    lane = iota((1, cap), 1)
    for copy in fetches[0:3]:
        copy.wait()
    for b in range(n):
        mine = nodes[b : b + 1, :] - b * node_rows
        group = jnp.zeros((1, cap), I32)
        for k in range(1, groups):
            group = group + jnp.where(mine >= k * rows_n, 1, 0)
        live = lane < counts[0:1, b : b + 1]
        place = jnp.where(live, mine - group * rows_n, rows_n)
        rest_of = ticks[b : b + 1, :] + jnp.where(live, group, groups) * (1 << SHIFT)
        for half in range(per):
            lanes = slice(half * LANES, (half + 1) * LANES)
            meta_src[b, half : half + 1, :] = place[:, lanes]
            meta_src[b, per + half : per + half + 1, :] = rest_of[:, lanes]

    pl.semaphore_wait(barrier, n + c - 2)
    metas = [
        remote(
            meta_src.at[mate(row, k, n)],
            meta.at[row],
            meta_s.at[0],
            meta_r.at[k],
            "rows",
            mate(row, k, n),
        )
        for k in range(1, n)
    ]
    for copy in reversed(metas):
        copy.start()
    meta[row] = meta_src[row]

    for copy in fetches[3:]:
        copy.wait()
    q = iota((1, LANES), 1)
    gate = jnp.zeros((1, LANES), I32)
    for k in range(1, 4):
        gate = gate + jnp.where(q >= k * wp, 1, 0)
    target = jnp.where(q < g3, 3 * (q - gate * wp) + gate, -width)
    stacked = jnp.concatenate([w_pair[:, 0, :], w_pair[:, 1, :], w_time[...], w_hid[...]], axis=0)
    from_col = iota((width, LANES), 0)
    for p in range(c):
        pick = jnp.where(from_col == target + p * g3, 1.0, 0.0).astype(B16)
        block = jnp.dot(stacked, pick, preferred_element_type=F32).astype(B16)
        for k in range(4):
            w_src[p, k] = block[k * wp : (k + 1) * wp]
    sends = [
        remote(
            w_src.at[mate(col, k, c)], w.at[col], w_s.at[0], w_r.at[0], "cols", mate(col, k, c)
        )
        for k in range(1, c)
    ]
    for copy in sends:
        copy.start()
    w[col] = w_src[col]

    rows[rows_n:, :] = jnp.zeros((8, LANES), F32)
    per_piece = step // LANES

    def turn(i, _):
        block = [flat[:, lanes_of(k * (rows_n // LANES) + i, LANES)] for k in range(groups)]
        rows[lanes_of(i, LANES), :] = jnp.concatenate(block, 0).T
        return 0

    for i in range(PIECES):
        all_groups = pl.ds(0, groups * step)
        pltpu.make_async_copy(
            memory.at[:, all_groups], flat.at[:, all_groups], load_sem.at[i]
        ).wait()
        lax.fori_loop(i * per_piece, (i + 1) * per_piece, turn, 0, unroll=8)

    sources = [mate(row, k, n, True) for k in range(n)]
    others = [mate(row, k, n) for k in range(n)]
    id_copies = [
        pltpu.make_async_copy(meta.at[sources[k]], ids.at[sources[k]], id_sem.at[k])
        for k in range(n)
    ]

    def arrive(k):
        if k:
            remote(
                meta_src.at[others[k]],
                meta.at[sources[k]],
                meta_s.at[0],
                meta_r.at[k],
                "rows",
                others[k],
            ).wait_recv()
        id_copies[k].start()

    def reply(k):
        b = sources[k]
        return remote(
            self_all.at[col, b], held.at[row], reply_s.at[0], reply_r.at[0], "rows", b
        )

    rest = pl.ds(0, n - 1)
    reply_in = remote(
        self_all.at[col, rest], held.at[rest], reply_s.at[0], reply_r.at[0], "rows", others[1]
    )

    begin_self, forward_self, finish_self, drain_self = ladder(
        c, self_all, lambda k: self_all.at[col, sources[k]], sources, SELF_PARTS, *hops[0:2]
    )
    begin, forward, finish, drain = ladder(
        c,
        part_all,
        lambda k: part_all.at[col, sources[k]] if k else perm.at[row],
        sources,
        n,
        *hops[2:4],
    )

    def gather(b):
        def slots(half, _):
            for u in range(LANES):
                picked[pl.ds(half * LANES + u, 1), :] = rows[pl.ds(ids[b, half, u], 1), :]
            return 0

        lax.fori_loop(0, per, slots, 0)
        for half in range(per):
            lanes = slice(half * LANES, (half + 1) * LANES)
            group = group_row(b, half)
            turned = picked[lanes, :].T
            mine = turned[0:wp]
            for k in range(1, groups):
                mine = jnp.where(group == k, turned[k * wp : (k + 1) * wp], mine)
            own[:, lanes_of(b * per + half, LANES)] = mine
            self_all[col, b, :, lanes] = mine.astype(B16)

    arrive(0)
    for k in range(n):
        if k + 1 < n:
            arrive(k + 1)
        id_copies[k].wait()
        gather(sources[k])
        if k:
            reply(k).start()
        else:
            held[row] = self_all[col, row]
        begin_self(k)

    hi_rows = node_rows // LANES
    old = last[...]
    table = jnp.concatenate(
        [lax.shift_right_logical(old, 8).astype(F32), lax.bitwise_and(old, 255).astype(F32)], axis=1
    ).astype(B16)
    hi_iota = iota((hi_rows, cap), 0)
    lo_iota = iota((LANES, cap), 0)

    def gap_of(b, _):
        node = wide_row(node_row, b)
        pick = jnp.where(hi_iota == lax.shift_right_logical(node, 7), 1.0, 0.0).astype(B16)
        found = over_in(table, pick)
        found = found[0:LANES] * 256.0 + found[LANES:]
        found = jnp.where(lo_iota == lax.bitwise_and(node, LANES - 1), found, 0.0)
        tick = wide_row(lambda b, half: meta[b, pl.ds(per + half, 1), :], b)
        tick = lax.bitwise_and(tick, (1 << SHIFT) - 1).astype(F32)
        gaps[b] = tick - jnp.sum(found, axis=0, keepdims=True)
        return 0

    lax.fori_loop(0, n, gap_of, 0, unroll=2)

    for k in range(tiles):
        half = slice((k % per) * LANES, (k % per + 1) * LANES)
        where[k : k + 1, :] = pair[k // per : k // per + 1, half]

    def column(i, _):
        block, half = lax.div(i, per), lax.rem(i, per)
        node = node_row(block, half).astype(F32)
        columns[lanes_of(i, LANES), :] = jnp.broadcast_to(node, (LANES, LANES)).T
        return 0

    lax.fori_loop(0, tiles, column, 0, unroll=4)

    reply_in.wait_recv()

    for k in range(tiles):
        wide[k] = held[k // per, :, (k % per) * LANES : (k % per + 1) * LANES].astype(F32)

    def permute(block, _):
        for half in range(per):
            p = where[pl.ds(block * per + half, 1), :]
            tile = jnp.broadcast_to(lax.shift_right_logical(p, 7), (8, LANES))
            place = jnp.broadcast_to(lax.bitwise_and(p, LANES - 1), (8, LANES))
            parts = [jnp.zeros((8, LANES), F32) for _ in range(wp // 8)]
            for k in range(tiles):
                hit = tile == k
                for r in range(wp // 8):
                    got = jnp.take_along_axis(wide[k, r * 8 : (r + 1) * 8, :], place, axis=1)
                    parts[r] = jnp.where(hit, got, parts[r])
            whole = jnp.concatenate(parts, axis=0).astype(B16)
            perm[block, :, half * LANES : (half + 1) * LANES] = whole
        return 0

    lax.fori_loop(0, n, permute, 0)

    spreads = [
        remote(
            perm.at[others[k]],
            part_all.at[col, row],
            spread_s.at[0],
            spread_r.at[k],
            "rows",
            others[k],
        )
        for k in range(1, n)
    ]
    for copy in spreads:
        copy.start()

    def spread_in(k):
        return remote(
            perm.at[others[k]],
            part_all.at[col, sources[k]],
            spread_s.at[0],
            spread_r.at[k],
            "rows",
            others[k],
        )

    begin(0)
    part_all[col, row] = perm[row]

    def same_of(i, _):
        block, half = lax.div(i, per), lax.rem(i, per)
        same = columns[...] == node_row(block, half).astype(F32)
        equal[:, lanes_of(i, LANES)] = jnp.where(same, 1.0, 0.0).astype(B16)
        return 0

    for k in range(n):
        lax.fori_loop(k * per, (k + 1) * per, same_of, 0)
        if (k + 1) % (n // SELF_PARTS) == 0:
            forward_self(k // (n // SELF_PARTS))
    for k in range(1, n):
        spread_in(k).wait_recv()
        begin(k)

    few = pl.ds(0, c - 1)
    w_in = remote(w_src.at[few], w.at[few], w_s.at[0], w_r.at[0], "cols", mate(col, 1, c))
    w_in.wait_recv()
    w_self, w_part, w_time_all, w_hid_all = (
        w[:, k].reshape(c * wp, LANES)[:, 0:g3] for k in range(4)
    )
    to_row = iota((g3, g3), 0)
    to_gate = jnp.zeros((g3, g3), I32)
    for k in range(1, 3):
        to_gate = to_gate + jnp.where(to_row >= k * wp, 1, 0)
    hit = iota((g3, g3), 1) == 3 * (to_row - to_gate * wp) + to_gate
    bias_x, bias_h = spread_row(bias_in, hit), spread_row(bias_hid, hit)
    square = (freq.shape[1],) * 2
    diagonal = iota(square, 0) == iota(square, 1)
    rate, shift_by = spread_row(freq, diagonal), spread_row(phase, diagonal)
    acc[...] = jnp.zeros(acc.shape, F32)
    number[...] = jnp.zeros(number.shape, F32)

    def time_part(b, _):
        encoded = jnp.cos(gaps[b] * rate + shift_by).astype(B16)
        timed[:, lanes_of(b, cap)] = over_in(w_time_all, encoded)
        return 0

    early = n // 2 + 1
    lax.fori_loop(0, early, time_part, 0)
    for k in range(early, n):
        forward(k - early)
        lax.fori_loop(k, k + 1, time_part, 0)

    for k in range(SELF_PARTS):
        finish_self(k)

    def self_part(b, _):
        lanes = lanes_of(b, cap)
        xs = self_all[:, b].reshape(c * wp, cap)
        gx = over_in(w_self, xs) + bias_x
        gh = over_in(w_hid_all, xs) + bias_h
        pre[0 : 2 * wp, lanes] = gx[0 : 2 * wp] + gh[0 : 2 * wp]
        pre[2 * wp : 3 * wp, lanes] = gx[2 * wp :]
        pre[3 * wp :, lanes] = gh[2 * wp :]
        return 0

    lax.fori_loop(0, n, self_part, 0, unroll=4)

    def add_block(k):
        b = sources[k]
        xp = part_all[:, b].reshape(c * wp, cap)
        gi = over_in(w_part, xp) + timed[:, lanes_of(b, cap)]
        big = gi.astype(B16)
        both = jnp.concatenate(
            [big, (gi - big.astype(F32)).astype(B16), jnp.ones((16, cap), B16)], axis=0
        )
        mine = pl.ds(pl.multiple_of(b * cap, cap), cap)

        def into(i, _):
            lanes = lanes_of(i, cap)
            sums = jnp.dot(both, equal[mine, lanes], preferred_element_type=F32)
            acc[:, lanes] += sums[0:g3] + sums[g3 : 2 * g3]
            number[:, lanes] += sums[2 * g3 : 2 * g3 + 8]
            return 0

        lax.fori_loop(0, n, into, 0, unroll=8)

    sent = n - early
    for k in range(n):
        ahead = min(k + sent, n)
        if k + sent < n:
            forward(ahead)
        finish(k)
        add_block(k)

    def gates(b, _):
        lanes = lanes_of(b, cap)
        mean = acc[:, lanes] * (1.0 / number[0:1, lanes])
        rz = jax.nn.sigmoid(mean[0 : 2 * wp] + pre[0 : 2 * wp, lanes])
        reset, keep = rz[0:wp], rz[wp:]
        cand = jnp.tanh(mean[2 * wp :] + pre[2 * wp : 3 * wp, lanes] + reset * pre[3 * wp :, lanes])
        fresh[:, lanes] = (1.0 - keep) * cand + keep * own[:, lanes]
        return 0

    lax.fori_loop(0, n, gates, 0)

    remote(
        meta_src.at[rest], meta.at[rest], meta_s.at[0], meta_r.at[0], "rows", others[1]
    ).wait_send()
    remote(perm.at[rest], perm.at[rest], spread_s.at[0], spread_r.at[0], "rows", others[1]).wait_send()
    w_in.wait_send()
    reply_in.wait_send()
    drain_self()
    drain()


def scatter_kernel(ids, meta, fresh, _, out, rows, flat, turned, group_at, out_sem):
    n, per = ids.shape[0], ids.shape[1] // 2
    wp, node_rows = out.shape
    groups = LANES // wp
    rows_n = node_rows // groups
    tiles = n * per
    step = rows_n // PIECES

    def tile(i, _):
        value = fresh[:, lanes_of(i, LANES)]
        turned[lanes_of(i, LANES), :] = jnp.concatenate([value] * groups, axis=0).T
        b, half = lax.div(i, per), lax.rem(i, per)
        group = lax.shift_right_logical(meta[b, pl.ds(per + half, 1), :], SHIFT).astype(F32)
        group_at[lanes_of(i, LANES), :] = jnp.broadcast_to(group, (LANES, LANES)).T
        return 0

    lax.fori_loop(0, tiles, tile, 0, unroll=4)
    group_of = lax.div(iota((1, LANES), 1), wp).astype(F32)

    def slots(i, _):
        b, half = lax.div(i, per), lax.rem(i, per)
        for u in range(LANES):
            pltpu.store(
                rows.at[pl.ds(ids[b, half, u], 1), :],
                turned[pl.ds(i * LANES + u, 1), :],
                mask=group_of == group_at[pl.ds(i * LANES + u, 1), :],
            )
        return 0

    lax.fori_loop(0, tiles, slots, 0)
    per_piece = step // LANES

    def back(i, _):
        x = rows[lanes_of(i, LANES), :].T
        for k in range(groups):
            flat[:, lanes_of(k * (rows_n // LANES) + i, LANES)] = x[k * wp : (k + 1) * wp]
        return 0

    copies = []
    for i in range(PIECES):
        lax.fori_loop(i * per_piece, (i + 1) * per_piece, back, 0, unroll=8)
        for k in range(groups):
            part = pl.ds(k * rows_n + i * step, step)
            copies.append(pltpu.make_async_copy(flat.at[:, part], out.at[:, part], out_sem))
            copies[-1].start()
    pltpu.make_async_copy(flat, out, out_sem).wait()


def dma(*shape):
    return pltpu.SemaphoreType.DMA(shape)


def local(
    n,
    c,
    memory,
    last_tick,
    slot_node,
    slot_pair,
    slot_tick,
    block_count,
    time_freq,
    time_phase,
    w_pair,
    w_time,
    w_hidden,
    bias_input,
    bias_hidden,
):
    wp, node_rows = memory.shape
    cap = slot_node.shape[1]
    total = n * cap
    tiles = total // LANES
    per = cap // LANES
    g3 = 3 * wp
    groups = LANES // wp
    rows_n = node_rows // groups
    shape = jax.ShapeDtypeStruct
    vm = pltpu.VMEM
    kept = 4 * ((rows_n + 8) * LANES + wp * total + 2 * total)
    limit = VMEM_BYTES - kept - (1 << 20)
    small = (
        slot_node,
        slot_tick,
        block_count,
        slot_pair,
        last_tick.reshape(node_rows // LANES, LANES),
        w_pair,
        w_time,
        w_hidden,
        bias_input.reshape(1, g3),
        bias_hidden.reshape(1, g3),
        time_freq.reshape(1, -1),
        time_phase.reshape(1, -1),
    )
    meta, fresh, rows = pl.pallas_call(
        functools.partial(main_kernel, n, c),
        out_shape=(
            vm((n, 2 * per, LANES), I32),
            vm((wp, total), F32),
            vm((rows_n + 8, LANES), F32),
        ),
        in_specs=[HBM] * 13,
        out_specs=(VM, VM, VM),
        scratch_shapes=[
            *(vm(x.shape, x.dtype) for x in small),
            dma(len(small)),
            vm((wp, node_rows), F32),
            pltpu.SMEM((n, 2 * per, LANES), I32),
            vm((n, 2 * per, LANES), I32),
            vm((c, 4, wp, LANES), B16),
            vm((c, 4, wp, LANES), B16),
            vm((cap, LANES), F32),
            vm((wp, total), F32),
            vm((n, wp, cap), B16),
            vm((tiles, wp, LANES), F32),
            vm((tiles, LANES), I32),
            vm((n, wp, cap), B16),
            vm((c, n, wp, cap), B16),
            vm((c, n, wp, cap), B16),
            vm((n, 1, cap), F32),
            vm((total, LANES), F32),
            vm((total, total), B16),
            vm((8, total), F32),
            vm((g3, total), F32),
            vm((4 * wp, total), F32),
            vm((g3, total), F32),
            dma(PIECES),
            dma(n),
            dma(1),
            dma(n),
            dma(1),
            dma(1),
            dma(1),
            dma(1),
            dma(1),
            dma(n),
            dma(2 * c),
            dma(c, SELF_PARTS),
            dma(2 * c),
            dma(c, n),
        ],
        compiler_params=pltpu.CompilerParams(
            collective_id=1, has_side_effects=True, vmem_limit_bytes=limit
        ),
        name="exchange",
    )(*(pltpu.with_memory_space_constraint(x, pltpu.HBM) for x in (*small, memory)))
    return pl.pallas_call(
        scatter_kernel,
        out_shape=(shape((wp, node_rows), F32), vm((rows_n + 8, LANES), F32)),
        in_specs=[SM, VM, VM, VM],
        out_specs=(ANY, VM),
        scratch_shapes=[
            vm((wp, node_rows), F32),
            vm((total, LANES), F32),
            vm((total, LANES), F32),
            pltpu.SemaphoreType.DMA,
        ],
        input_output_aliases={3: 1},
        compiler_params=pltpu.CompilerParams(vmem_limit_bytes=4 * (wp * node_rows + 2 * total * LANES) + (6 << 20)),
        name="scatter",
    )(meta, meta, fresh, rows)[0]


def solution(mesh):
    placed = (
        P("cols", "rows"),
        P("rows"),
        P("rows", None),
        P("rows", None),
        P("rows", None),
        P("rows", None),
        P(),
        P(),
        P("cols", None, None),
        P("cols", None),
        P("cols", None),
        P("cols"),
        P("cols"),
    )
    return jax.shard_map(
        functools.partial(local, mesh.shape["rows"], mesh.shape["cols"]),
        mesh=mesh,
        in_specs=placed,
        out_specs=P("cols", "rows"),
        check_vma=False,
    )
```

time: 64.6 us -> 38.4 us (0.59)
  Pallas kernels: 64.3 us -> 38.3 us
    pallas_call x2, Pallas kernels: 64.3 us -> 38.3 us  [the longest x1 32.2 us: local(): pl.pallas_call(functools.partial(main_kernel, n, c), out_shape=(vm((n, 2...]
where the time goes in v2:
time: 38.4 us; the launch traced here: 38.3 us
  Pallas kernels  38.3 us (100%)
    pallas_call x1, Pallas kernels, local(): pl.pallas_call(functools.partial(main_kernel, n, c), out_shape=(vm((n, 2...  32.2 us
    pallas_call x1, Pallas kernels, local(): pl.pallas_call(scatter_kernel, out_shape=(shape((wp, node_rows), F32), vm...  6.07 us

profile of v2, /device:TPU:0, one launch (start us, length us, event | category | flops | bytes accessed | tf_op | source)
XLA Modules:
  0.0 38.3 jit_solution(10955979903359013418)
XLA Ops:
  0.0 32.2 %exchange.1 = (s32[8,4,128]{2,1,0:T(4,128)S(1)}, f32[32,2048]{1,0:T(8,128)S(1)}, f32[8200,128]{1,0:T(8,128)S(1)}) custom-call(s32[8,256]{1,0:T(8,128)} %refs_0_.1, s32[8,256]{1,0:T(8,128)} %refs_1_.1, s32[1,8]{1,0:T(1,128)} %refs_2_.1, s32[8,256]{1,0:T(8,128)} %refs_3_.1, s32[256,128]{1,0:T(8,128)} %bitcast.5, bf16[32,2,384]{2,1,0:T(2,128)(2,1)} %refs_5_.1, ...), custom_call_target="tpu_custom_call" | custom-call | tf_op jit(solution)/shard_map/exchange/pallas_call | solution.py:670
  32.2 6.1 %scatter.1 = (f32[32,32768]{1,0:T(8,128)}, f32[8200,128]{1,0:T(8,128)S(1)}) custom-call(s32[8,4,128]{2,1,0:T(4,128)S(1)} %get-tuple-element.9.ids.meta, s32[8,4,128]{2,1,0:T(4,128)S(1)} %get-tuple-element.9.ids.meta, f32[32,2048]{1,0:T(8,128)S(1)} %get-tuple-element.10.fresh, f32[8200,128]{1,0:T(8,128)S(1)} %get-tuple-element.11._), custom_call_target="tpu_custom_call", output_to_operand_aliasing={{1}: (3, {})} | custom-call | tf_op jit(solution)/shard_map/scatter/pallas_call | solution.py:722

commit v3 on v2

--- a/solution.py
+++ b/solution.py
@@ -1,4 +1,5 @@
 import functools
+import math
 
 import jax
 import jax.numpy as jnp
@@ -16,7 +17,7 @@
 HBM = pl.BlockSpec(memory_space=pltpu.HBM)
 PIECES = 4
 VMEM_BYTES = 67_043_328
-SELF_PARTS = 2
+SELF_PARTS = 4
 F32, I32, B16 = jnp.float32, jnp.int32, jnp.bfloat16
 
 
@@ -57,7 +58,10 @@
         return towards(d, right) < c if right else towards(d, right) >= 0
 
     def send_sem(d, right):
-        return sends.at[2 * d + right]
+        return sends.at[2 * d + right - 2]
+
+    def slot(source, target):
+        return lax.rem(source - target + c, c) - 1
 
     def hop(d, k, right, stride):
         source = towards(stride - d, right)
@@ -66,7 +70,7 @@
             first(k) if d == stride else ref,
             ref,
             send_sem(d, right),
-            recvs.at[source, k // each],
+            recvs.at[slot(source, towards(stride, right)), k // each],
             "cols",
             towards(stride, right),
         )
@@ -75,7 +79,7 @@
         source = towards(-d, right)
         peer = jnp.minimum(col + 1, c - 1) if right else jnp.maximum(col - 1, 0)
         ref = buffer.at[source, pl.ds(0, each)]
-        return remote(ref, ref, send_sem(d, right), recvs.at[source, part], "cols", peer)
+        return remote(ref, ref, send_sem(d, right), recvs.at[slot(source, col), part], "cols", peer)
 
     def when(*tests):
         return pl.when(functools.reduce(jnp.logical_and, tests))
@@ -139,18 +143,31 @@
     return lax.dot_general(a, b, (((0,), (0,)), ((), ())), preferred_element_type=F32)
 
 
+SINE = [(-1) ** i * (2.0 * math.pi) ** (2 * i + 1) / math.factorial(2 * i + 1) for i in range(7)]
+
+
+def cos_turns(x):
+    big = 1.5 * 2.0**23
+    x = 0.25 - jnp.abs(x - ((x + big) - big))
+    square = x * x
+    out = jnp.full_like(x, SINE[-1])
+    for term in SINE[-2::-1]:
+        out = out * square + term
+    return out * x
+
+
 def iota(shape, axis):
     return lax.broadcasted_iota(I32, shape, axis)
 
 
 def main_kernel(n, c, *refs):
     given, memory, refs = refs[0:12], refs[12], refs[13:]
-    meta, fresh, rows, refs = *refs[0:3], refs[3:]
+    outs, refs = refs[0:4], refs[4:]
     taken, in_sem, refs = refs[0:12], refs[12], refs[13:]
     fetches = [
         pltpu.make_async_copy(a, b, in_sem.at[i]) for i, (a, b) in enumerate(zip(given, taken))
     ]
-    main_body(n, c, fetches, *taken, memory, meta, fresh, rows, *refs)
+    main_body(n, c, fetches, *taken, memory, *outs, *refs)
 
 
 def main_body(
@@ -173,12 +190,14 @@
     meta,
     fresh,
     rows,
+    columns,
     flat,
     ids,
     meta_src,
     w_src,
     w,
-    picked,
+    picked_0,
+    picked_1,
     own,
     held,
     wide,
@@ -187,7 +206,6 @@
     self_all,
     part_all,
     gaps,
-    columns,
     equal,
     number,
     timed,
@@ -206,6 +224,7 @@
     *hops,
 ):
     row, col = lax.axis_index("rows"), lax.axis_index("cols")
+    picked = (picked_0, picked_1)
     cap = nodes.shape[1]
     wp, node_rows = memory.shape
     groups = LANES // wp
@@ -274,53 +293,17 @@
         copy.start()
     meta[row] = meta_src[row]
 
-    for copy in fetches[3:]:
-        copy.wait()
-    q = iota((1, LANES), 1)
-    gate = jnp.zeros((1, LANES), I32)
-    for k in range(1, 4):
-        gate = gate + jnp.where(q >= k * wp, 1, 0)
-    target = jnp.where(q < g3, 3 * (q - gate * wp) + gate, -width)
-    stacked = jnp.concatenate([w_pair[:, 0, :], w_pair[:, 1, :], w_time[...], w_hid[...]], axis=0)
-    from_col = iota((width, LANES), 0)
-    for p in range(c):
-        pick = jnp.where(from_col == target + p * g3, 1.0, 0.0).astype(B16)
-        block = jnp.dot(stacked, pick, preferred_element_type=F32).astype(B16)
-        for k in range(4):
-            w_src[p, k] = block[k * wp : (k + 1) * wp]
-    sends = [
-        remote(
-            w_src.at[mate(col, k, c)], w.at[col], w_s.at[0], w_r.at[0], "cols", mate(col, k, c)
-        )
-        for k in range(1, c)
-    ]
-    for copy in sends:
-        copy.start()
-    w[col] = w_src[col]
-
-    rows[rows_n:, :] = jnp.zeros((8, LANES), F32)
-    per_piece = step // LANES
-
-    def turn(i, _):
-        block = [flat[:, lanes_of(k * (rows_n // LANES) + i, LANES)] for k in range(groups)]
-        rows[lanes_of(i, LANES), :] = jnp.concatenate(block, 0).T
-        return 0
-
-    for i in range(PIECES):
-        all_groups = pl.ds(0, groups * step)
-        pltpu.make_async_copy(
-            memory.at[:, all_groups], flat.at[:, all_groups], load_sem.at[i]
-        ).wait()
-        lax.fori_loop(i * per_piece, (i + 1) * per_piece, turn, 0, unroll=8)
-
     sources = [mate(row, k, n, True) for k in range(n)]
     others = [mate(row, k, n) for k in range(n)]
+    order = [0, 1, 2, *range(n - 1, 2, -1)]
+    turns_of = [sources[k] for k in order]
     id_copies = [
-        pltpu.make_async_copy(meta.at[sources[k]], ids.at[sources[k]], id_sem.at[k])
-        for k in range(n)
+        pltpu.make_async_copy(meta.at[b], ids.at[b], id_sem.at[i % 3])
+        for i, b in enumerate(turns_of)
     ]
 
-    def arrive(k):
+    def arrive(i):
+        k = order[i]
         if k:
             remote(
                 meta_src.at[others[k]],
@@ -330,7 +313,48 @@
                 "rows",
                 others[k],
             ).wait_recv()
-        id_copies[k].start()
+        id_copies[i].start()
+
+    arrive(0)
+    rows[rows_n:, :] = jnp.zeros((8, LANES), F32)
+    per_piece = step // LANES
+
+    def turn(i, _):
+        block = [flat[:, lanes_of(k * (rows_n // LANES) + i, LANES)] for k in range(groups)]
+        rows[lanes_of(i, LANES), :] = jnp.concatenate(block, 0).T
+        return 0
+
+    for i in range(PIECES):
+        if i == 1:
+            for copy in fetches[3:]:
+                copy.wait()
+            q = iota((1, LANES), 1)
+            gate = jnp.zeros((1, LANES), I32)
+            for k in range(1, 4):
+                gate = gate + jnp.where(q >= k * wp, 1, 0)
+            target = jnp.where(q < g3, 3 * (q - gate * wp) + gate, -width)
+            stacked = jnp.concatenate([w_pair[:, 0, :], w_pair[:, 1, :], w_time[...], w_hid[...]], axis=0)
+            from_col = iota((width, LANES), 0)
+            for p in range(c):
+                pick = jnp.where(from_col == target + p * g3, 1.0, 0.0).astype(B16)
+                block = jnp.dot(stacked, pick, preferred_element_type=F32)
+                kinds = [block[k * wp : (k + 1) * wp, 0:g3] for k in range(4)]
+                w_src[p] = jnp.concatenate(kinds, axis=1).astype(B16)
+            sends = [
+                remote(
+                    w_src.at[mate(col, k, c)], w.at[col], w_s.at[0], w_r.at[0], "cols", mate(col, k, c)
+                )
+                for k in range(1, c)
+            ]
+            for copy in sends:
+                copy.start()
+            w[col] = w_src[col]
+
+        all_groups = pl.ds(0, groups * step)
+        pltpu.make_async_copy(
+            memory.at[:, all_groups], flat.at[:, all_groups], load_sem.at[i]
+        ).wait()
+        lax.fori_loop(i * per_piece, (i + 1) * per_piece, turn, 0, unroll=16)
 
     def reply(k):
         b = sources[k]
@@ -344,7 +368,7 @@
     )
 
     begin_self, forward_self, finish_self, drain_self = ladder(
-        c, self_all, lambda k: self_all.at[col, sources[k]], sources, SELF_PARTS, *hops[0:2]
+        c, self_all, lambda i: self_all.at[col, turns_of[i]], turns_of, SELF_PARTS, *hops[0:2]
     )
     begin, forward, finish, drain = ladder(
         c,
@@ -355,55 +379,43 @@
         *hops[2:4],
     )
 
-    def gather(b):
-        def slots(half, _):
+    def slots(i):
+        b = turns_of[i]
+        for half in range(per):
             for u in range(LANES):
-                picked[pl.ds(half * LANES + u, 1), :] = rows[pl.ds(ids[b, half, u], 1), :]
-            return 0
-
-        lax.fori_loop(0, per, slots, 0)
+                r = ids[b, half, u]
+                picked[i % 2][half * LANES + u : half * LANES + u + 1, :] = rows[pl.ds(r, 1), :]
+
+    def turn_back(i):
+        b = turns_of[i]
         for half in range(per):
             lanes = slice(half * LANES, (half + 1) * LANES)
             group = group_row(b, half)
-            turned = picked[lanes, :].T
+            turned = picked[i % 2][lanes, :].T
             mine = turned[0:wp]
-            for k in range(1, groups):
-                mine = jnp.where(group == k, turned[k * wp : (k + 1) * wp], mine)
+            for g in range(1, groups):
+                mine = jnp.where(group == g, turned[g * wp : (g + 1) * wp], mine)
             own[:, lanes_of(b * per + half, LANES)] = mine
             self_all[col, b, :, lanes] = mine.astype(B16)
 
-    arrive(0)
-    for k in range(n):
-        if k + 1 < n:
-            arrive(k + 1)
-        id_copies[k].wait()
-        gather(sources[k])
-        if k:
-            reply(k).start()
+    def send_own(i):
+        if order[i]:
+            reply(order[i]).start()
         else:
             held[row] = self_all[col, row]
-        begin_self(k)
-
-    hi_rows = node_rows // LANES
-    old = last[...]
-    table = jnp.concatenate(
-        [lax.shift_right_logical(old, 8).astype(F32), lax.bitwise_and(old, 255).astype(F32)], axis=1
-    ).astype(B16)
-    hi_iota = iota((hi_rows, cap), 0)
-    lo_iota = iota((LANES, cap), 0)
-
-    def gap_of(b, _):
-        node = wide_row(node_row, b)
-        pick = jnp.where(hi_iota == lax.shift_right_logical(node, 7), 1.0, 0.0).astype(B16)
-        found = over_in(table, pick)
-        found = found[0:LANES] * 256.0 + found[LANES:]
-        found = jnp.where(lo_iota == lax.bitwise_and(node, LANES - 1), found, 0.0)
-        tick = wide_row(lambda b, half: meta[b, pl.ds(per + half, 1), :], b)
-        tick = lax.bitwise_and(tick, (1 << SHIFT) - 1).astype(F32)
-        gaps[b] = tick - jnp.sum(found, axis=0, keepdims=True)
-        return 0
-
-    lax.fori_loop(0, n, gap_of, 0, unroll=2)
+        begin_self(i)
+
+    arrive(1)
+    for i in range(n):
+        if i + 2 < n:
+            arrive(i + 2)
+        id_copies[i].wait()
+        slots(i)
+        if i:
+            turn_back(i - 1)
+            send_own(i - 1)
+    turn_back(n - 1)
+    send_own(n - 1)
 
     for k in range(tiles):
         half = slice((k % per) * LANES, (k % per + 1) * LANES)
@@ -417,12 +429,13 @@
 
     lax.fori_loop(0, tiles, column, 0, unroll=4)
 
+    forward_self(0)
     reply_in.wait_recv()
 
     for k in range(tiles):
         wide[k] = held[k // per, :, (k % per) * LANES : (k % per + 1) * LANES].astype(F32)
 
-    def permute(block, _):
+    def permute(block):
         for half in range(per):
             p = where[pl.ds(block * per + half, 1), :]
             tile = jnp.broadcast_to(lax.shift_right_logical(p, 7), (8, LANES))
@@ -435,12 +448,9 @@
                     parts[r] = jnp.where(hit, got, parts[r])
             whole = jnp.concatenate(parts, axis=0).astype(B16)
             perm[block, :, half * LANES : (half + 1) * LANES] = whole
-        return 0
-
-    lax.fori_loop(0, n, permute, 0)
-
-    spreads = [
-        remote(
+
+    def spread_out(k):
+        return remote(
             perm.at[others[k]],
             part_all.at[col, row],
             spread_s.at[0],
@@ -448,10 +458,13 @@
             "rows",
             others[k],
         )
-        for k in range(1, n)
-    ]
-    for copy in spreads:
-        copy.start()
+
+    permute(row)
+    begin(0)
+    part_all[col, row] = perm[row]
+    for k in range(n - 1, 0, -1):
+        permute(others[k])
+        spread_out(k).start()
 
     def spread_in(k):
         return remote(
@@ -463,8 +476,6 @@
             others[k],
         )
 
-    begin(0)
-    part_all[col, row] = perm[row]
 
     def same_of(i, _):
         block, half = lax.div(i, per), lax.rem(i, per)
@@ -472,19 +483,48 @@
         equal[:, lanes_of(i, LANES)] = jnp.where(same, 1.0, 0.0).astype(B16)
         return 0
 
+    def pass_on(k):
+        spread_in(k).wait_recv()
+        begin(k)
+
+    first_in = n // 4
     for k in range(n):
         lax.fori_loop(k * per, (k + 1) * per, same_of, 0)
-        if (k + 1) % (n // SELF_PARTS) == 0:
-            forward_self(k // (n // SELF_PARTS))
-    for k in range(1, n):
-        spread_in(k).wait_recv()
-        begin(k)
-
+        if k == first_in - 1:
+            forward_self(1)
+        if k >= first_in:
+            pass_on(k - first_in + 1)
+    forward_self(2)
+    for k in range(n - first_in + 1, n):
+        pass_on(k)
+
+    hi_rows = node_rows // LANES
+    old = last[...]
+    table = jnp.concatenate(
+        [lax.shift_right_logical(old, 8).astype(F32), lax.bitwise_and(old, 255).astype(F32)], axis=1
+    ).astype(B16)
+    hi_iota = iota((hi_rows, cap), 0)
+    lo_iota = iota((LANES, cap), 0)
+
+    def gap_of(b, _):
+        node = wide_row(node_row, b)
+        pick = jnp.where(hi_iota == lax.shift_right_logical(node, 7), 1.0, 0.0).astype(B16)
+        found = over_in(table, pick)
+        found = found[0:LANES] * 256.0 + found[LANES:]
+        found = jnp.where(lo_iota == lax.bitwise_and(node, LANES - 1), found, 0.0)
+        tick = wide_row(lambda b, half: meta[b, pl.ds(per + half, 1), :], b)
+        tick = lax.bitwise_and(tick, (1 << SHIFT) - 1).astype(F32)
+        gaps[b] = tick - jnp.sum(found, axis=0, keepdims=True)
+        return 0
+
+    lax.fori_loop(0, n, gap_of, 0, unroll=2)
+
+    forward_self(3)
     few = pl.ds(0, c - 1)
     w_in = remote(w_src.at[few], w.at[few], w_s.at[0], w_r.at[0], "cols", mate(col, 1, c))
     w_in.wait_recv()
     w_self, w_part, w_time_all, w_hid_all = (
-        w[:, k].reshape(c * wp, LANES)[:, 0:g3] for k in range(4)
+        w[...].reshape(c * wp, 4 * g3)[:, k * g3 : (k + 1) * g3] for k in range(4)
     )
     to_row = iota((g3, g3), 0)
     to_gate = jnp.zeros((g3, g3), I32)
@@ -494,20 +534,18 @@
     bias_x, bias_h = spread_row(bias_in, hit), spread_row(bias_hid, hit)
     square = (freq.shape[1],) * 2
     diagonal = iota(square, 0) == iota(square, 1)
-    rate, shift_by = spread_row(freq, diagonal), spread_row(phase, diagonal)
+    turns = 1.0 / (2.0 * math.pi)
+    rate = spread_row(freq, diagonal) * turns
+    shift_by = spread_row(phase, diagonal) * turns
     acc[...] = jnp.zeros(acc.shape, F32)
     number[...] = jnp.zeros(number.shape, F32)
 
     def time_part(b, _):
-        encoded = jnp.cos(gaps[b] * rate + shift_by).astype(B16)
+        encoded = cos_turns(gaps[b] * rate + shift_by).astype(B16)
         timed[:, lanes_of(b, cap)] = over_in(w_time_all, encoded)
         return 0
 
-    early = n // 2 + 1
-    lax.fori_loop(0, early, time_part, 0)
-    for k in range(early, n):
-        forward(k - early)
-        lax.fori_loop(k, k + 1, time_part, 0)
+    lax.fori_loop(0, n, time_part, 0, unroll=2)
 
     for k in range(SELF_PARTS):
         finish_self(k)
@@ -543,13 +581,13 @@
 
         lax.fori_loop(0, n, into, 0, unroll=8)
 
-    sent = n - early
-    for k in range(n):
-        ahead = min(k + sent, n)
-        if k + sent < n:
-            forward(ahead)
-        finish(k)
-        add_block(k)
+    lag = 2
+    for k in range(n + lag):
+        if k < n:
+            forward(k)
+        if k >= lag:
+            finish(k - lag)
+            add_block(k - lag)
 
     def gates(b, _):
         lanes = lanes_of(b, cap)
@@ -572,36 +610,39 @@
     drain()
 
 
-def scatter_kernel(ids, meta, fresh, _, out, rows, flat, turned, group_at, out_sem):
-    n, per = ids.shape[0], ids.shape[1] // 2
+def scatter_kernel(meta, fresh, columns, _, out, rows, flat, ids, turned, id_sem, out_sem):
+    n, per = meta.shape[0], meta.shape[1] // 2
     wp, node_rows = out.shape
     groups = LANES // wp
     rows_n = node_rows // groups
     tiles = n * per
-    step = rows_n // PIECES
-
-    def tile(i, _):
-        value = fresh[:, lanes_of(i, LANES)]
-        turned[lanes_of(i, LANES), :] = jnp.concatenate([value] * groups, axis=0).T
-        b, half = lax.div(i, per), lax.rem(i, per)
-        group = lax.shift_right_logical(meta[b, pl.ds(per + half, 1), :], SHIFT).astype(F32)
-        group_at[lanes_of(i, LANES), :] = jnp.broadcast_to(group, (LANES, LANES)).T
-        return 0
-
-    lax.fori_loop(0, tiles, tile, 0, unroll=4)
-    group_of = lax.div(iota((1, LANES), 1), wp).astype(F32)
-
-    def slots(i, _):
-        b, half = lax.div(i, per), lax.rem(i, per)
-        for u in range(LANES):
+    step = rows_n // (2 * PIECES)
+    copy = pltpu.make_async_copy(meta, ids, id_sem)
+    copy.start()
+
+    start = lax.div(iota((1, LANES), 1), wp).astype(F32) * rows_n
+    end = start + rows_n
+
+    def turn(i):
+        if i < tiles:
+            lanes = slice(i * LANES, (i + 1) * LANES)
+            turned[lanes, :] = jnp.concatenate([fresh[:, lanes]] * groups, axis=0).T
+
+    ahead = 4
+    for i in range(ahead):
+        turn(i)
+    copy.wait()
+    for i in range(tiles):
+        turn(i + ahead)
+        b, half = i // per, i % per
+        for u in range(i * LANES, (i + 1) * LANES):
+            node = columns[u : u + 1, :]
             pltpu.store(
-                rows.at[pl.ds(ids[b, half, u], 1), :],
-                turned[pl.ds(i * LANES + u, 1), :],
-                mask=group_of == group_at[pl.ds(i * LANES + u, 1), :],
+                rows.at[pl.ds(ids[b, half, u % LANES], 1), :],
+                turned[u : u + 1, :],
+                mask=jnp.logical_and(node >= start, node < end),
             )
-        return 0
-
-    lax.fori_loop(0, tiles, slots, 0)
+
     per_piece = step // LANES
 
     def back(i, _):
@@ -611,7 +652,7 @@
         return 0
 
     copies = []
-    for i in range(PIECES):
+    for i in range(2 * PIECES):
         lax.fori_loop(i * per_piece, (i + 1) * per_piece, back, 0, unroll=8)
         for k in range(groups):
             part = pl.ds(k * rows_n + i * step, step)
@@ -651,7 +692,7 @@
     rows_n = node_rows // groups
     shape = jax.ShapeDtypeStruct
     vm = pltpu.VMEM
-    kept = 4 * ((rows_n + 8) * LANES + wp * total + 2 * total)
+    kept = 4 * ((rows_n + 8) * LANES + wp * total + 2 * total + total * LANES)
     limit = VMEM_BYTES - kept - (1 << 20)
     small = (
         slot_node,
@@ -667,23 +708,25 @@
         time_freq.reshape(1, -1),
         time_phase.reshape(1, -1),
     )
-    meta, fresh, rows = pl.pallas_call(
+    meta, fresh, rows, columns = pl.pallas_call(
         functools.partial(main_kernel, n, c),
         out_shape=(
             vm((n, 2 * per, LANES), I32),
             vm((wp, total), F32),
             vm((rows_n + 8, LANES), F32),
+            vm((total, LANES), F32),
         ),
         in_specs=[HBM] * 13,
-        out_specs=(VM, VM, VM),
+        out_specs=(VM, VM, VM, VM),
         scratch_shapes=[
             *(vm(x.shape, x.dtype) for x in small),
             dma(len(small)),
             vm((wp, node_rows), F32),
             pltpu.SMEM((n, 2 * per, LANES), I32),
             vm((n, 2 * per, LANES), I32),
-            vm((c, 4, wp, LANES), B16),
-            vm((c, 4, wp, LANES), B16),
+            vm((c, wp, 4 * g3), B16),
+            vm((c, wp, 4 * g3), B16),
+            vm((cap, LANES), F32),
             vm((cap, LANES), F32),
             vm((wp, total), F32),
             vm((n, wp, cap), B16),
@@ -693,14 +736,13 @@
             vm((c, n, wp, cap), B16),
             vm((c, n, wp, cap), B16),
             vm((n, 1, cap), F32),
-            vm((total, LANES), F32),
             vm((total, total), B16),
             vm((8, total), F32),
             vm((g3, total), F32),
             vm((4 * wp, total), F32),
             vm((g3, total), F32),
             dma(PIECES),
-            dma(n),
+            dma(3),
             dma(1),
             dma(n),
             dma(1),
@@ -709,10 +751,10 @@
             dma(1),
             dma(1),
             dma(n),
-            dma(2 * c),
-            dma(c, SELF_PARTS),
-            dma(2 * c),
-            dma(c, n),
+            dma(2 * c - 2),
+            dma(c - 1, SELF_PARTS),
+            dma(2 * c - 2),
+            dma(c - 1, n),
         ],
         compiler_params=pltpu.CompilerParams(
             collective_id=1, has_side_effects=True, vmem_limit_bytes=limit
@@ -722,18 +764,19 @@
     return pl.pallas_call(
         scatter_kernel,
         out_shape=(shape((wp, node_rows), F32), vm((rows_n + 8, LANES), F32)),
-        in_specs=[SM, VM, VM, VM],
+        in_specs=[VM, VM, VM, VM],
         out_specs=(ANY, VM),
         scratch_shapes=[
             vm((wp, node_rows), F32),
+            pltpu.SMEM((n, 2 * per, LANES), I32),
             vm((total, LANES), F32),
-            vm((total, LANES), F32),
+            pltpu.SemaphoreType.DMA,
             pltpu.SemaphoreType.DMA,
         ],
         input_output_aliases={3: 1},
-        compiler_params=pltpu.CompilerParams(vmem_limit_bytes=4 * (wp * node_rows + 2 * total * LANES) + (6 << 20)),
+        compiler_params=pltpu.CompilerParams(vmem_limit_bytes=4 * (wp * node_rows + total * LANES) + (6 << 20)),
         name="scatter",
-    )(meta, meta, fresh, rows)[0]
+    )(meta, fresh, columns, rows)[0]
 
 
 def solution(mesh):

time: 38.4 us -> 35 us (0.911)
  Pallas kernels: 38.3 us -> 34.9 us
    pallas_call x1, Pallas kernels: 6.07 us -> 4.33 us  [local(): pl.pallas_call(scatter_kernel, out_shape=(shape((wp, node_rows), F32), vm...]
    pallas_call x1, Pallas kernels: 32.2 us -> 30.6 us  [local(): pl.pallas_call(functools.partial(main_kernel, n, c), out_shape=(vm((n, 2...]
where the time goes in v3:
time: 35 us; the launch traced here: 34.9 us
  Pallas kernels  34.9 us (100%)
    pallas_call x1, Pallas kernels, local(): pl.pallas_call(functools.partial(main_kernel, n, c), out_shape=(vm((n, 2...  30.6 us
    pallas_call x1, Pallas kernels, local(): pl.pallas_call(scatter_kernel, out_shape=(shape((wp, node_rows), F32), vm...  4.33 us

profile of v3, /device:TPU:0, one launch (start us, length us, event | category | flops | bytes accessed | tf_op | source)
XLA Modules:
  0.0 34.9 jit_solution(1684474825328420413)
XLA Ops:
  0.0 30.6 %exchange.1 = (s32[8,4,128]{2,1,0:T(4,128)S(1)}, f32[32,2048]{1,0:T(8,128)S(1)}, f32[8200,128]{1,0:T(8,128)S(1)}, f32[2048,128]{1,0:T(8,128)S(1)}) custom-call(s32[8,256]{1,0:T(8,128)} %refs_0_.1, s32[8,256]{1,0:T(8,128)} %refs_1_.1, s32[1,8]{1,0:T(1,128)} %refs_2_.1, s32[8,256]{1,0:T(8,128)} %refs_3_.1, s32[256,128]{1,0:T(8,128)} %bitcast.5, ...), custom_call_target="tpu_custom_call" | custom-call | tf_op jit(solution)/shard_map/exchange/pallas_call | solution.py:711
  30.6 4.3 %scatter.1 = (f32[32,32768]{1,0:T(8,128)}, f32[8200,128]{1,0:T(8,128)S(1)}) custom-call(s32[8,4,128]{2,1,0:T(4,128)S(1)} %get-tuple-element.10.meta, f32[32,2048]{1,0:T(8,128)S(1)} %get-tuple-element.11.fresh, f32[2048,128]{1,0:T(8,128)S(1)} %get-tuple-element.12.columns, f32[8200,128]{1,0:T(8,128)S(1)} %get-tuple-element.13._), custom_call_target="tpu_custom_call", output_to_operand_aliasing={{1}: (3, {})} | custom-call | tf_op jit(solution)/shard_map/scatter/pallas_call | solution.py:764
